TPU v7x, 512 devices: a whole 4x8x8 slice. The times are simulated.
512 devices in a mesh: owner: 64 (over z, x, core), rep: 8 (over y).
Axes of the slice: x: 4, y: 8, z: 8, core: 2. Of those that a mesh axis runs over, the one named last changes fastest.
Arguments:
- features: float32 [262144, 256], P(('owner', 'rep')), may hold values from -6 to 6
- group_ids: int32 [262144], P(('owner', 'rep')), may hold values from 0 to 65535, as said below
- survive: int32 [262144], P(('owner', 'rep')), may hold values from 0 to 1
- home_row: int32 [65536], replicated, may hold values from 0 to 65535, as said below
- hot_ids: int32 [256], replicated, may hold values from 0 to 65535, as said below
Outputs:
- group_out: float32 [65536, 256], P(('owner', 'rep'))
- group_count: float32 [65536], P(('owner', 'rep'))
- hot_out: float32 [256, 256], P('rep')
- hot_count: float32 [256], P('rep')
Inputs may be any that keep to these rules, and one draw needn't show every extreme that they name: home_row is a permutation of the groups. hot_ids holds 256 different groups. `group_ids`: among the rows of one device, 128 name hot groups, and at most 16 rows name non-hot groups g whose home_row[g] // 1024 is one and the same owner index; on every device some owners get exactly 16 such rows.
All inputs are finite; a program needn't handle non-finite values.
Results may differ from a plain program's by a relative error of at most 0.00007.
Values sent between devices are 32-bit elements; how exact they have to be, the bound alone decides.
A program may use at most 64 MiB of HBM per device.

v0:
```python
import math

import jax
import jax.numpy as jnp
from jax import lax
from jax.sharding import Mesh
from jax.sharding import PartitionSpec as P

OWNER = ("owner_0", "owner_1", "owner_2")
OWNER_REP = ("owner_0", "owner_1", "owner_2", "rep")


def split_up(shard, dim, devices):
    before, after = (shard.shape[:dim], shard.shape[dim + 1 :])
    return jnp.moveaxis(shard.reshape(*before, devices, -1, *after), dim, 0)


def sent_and_summed(shard, axis, dim):
    devices = lax.axis_size(axis)
    parts = lax.all_to_all(split_up(shard, dim, devices), axis, 0, 0, tiled=True)
    return jnp.sum(parts, axis=0)


def in_one_piece(arrays, axis, dim, along):
    columns = [a.reshape(*a.shape[:along], -1) for a in arrays]
    both = jnp.concatenate(columns, axis=along)
    out, at, done = (sent_and_summed(both, axis, dim), 0, [])
    for a, column in zip(arrays, columns):
        slab = out[..., at : at + column.shape[along]]
        done.append(slab.reshape(*slab.shape[:along], *a.shape[along:]))
        at += column.shape[along]
    return tuple(done)


def one_axis_at_a_time(shard, axes):
    for axis in axes:
        shard = lax.psum(shard, axis)
    return shard


def sent_together(arrays, axis, split_dim, concat_dim, along):
    widths = [math.prod(a.shape[along:]) for a in arrays]
    both = jnp.concatenate(
        [a.reshape(*a.shape[:along], w) for a, w in zip(arrays, widths)], axis=along
    )
    out = lax.all_to_all(both, axis, split_axis=split_dim, concat_axis=concat_dim, tiled=True)
    parts = jnp.split(out, [sum(widths[:k]) for k in range(1, len(widths))], axis=along)
    return tuple((b.reshape(*out.shape[:along], *a.shape[along:]) for a, b in zip(arrays, parts)))


def local(features, group_ids, survive, home_row, hot_ids):
    rows = features.shape[0]
    width = features.shape[1]
    owners = lax.axis_size(OWNER)
    own_groups = home_row.shape[0] // owners
    capacity = 2 * rows // owners
    live = survive == 1
    matches = group_ids[:, None] == hot_ids[None, :]
    is_hot = jnp.any(matches, axis=1)
    hot_table = jnp.where(matches & live[:, None], 1.0, 0.0).astype(jnp.float32)
    hot_part = lax.dot_general(
        hot_table,
        features,
        (((0,), (0,)), ((), ())),
        precision=lax.Precision.HIGHEST,
        preferred_element_type=jnp.float32,
    )
    hot_tally = jnp.sum(hot_table, axis=0)
    part_sum, part_tally = in_one_piece((hot_part, hot_tally), "rep", 0, 1)
    hot_sum, hot_count = (
        one_axis_at_a_time(part_sum, OWNER),
        one_axis_at_a_time(part_tally, OWNER),
    )
    hot_out = hot_sum / jnp.sqrt(1.0 + hot_count)[:, None]
    keep = live & jnp.logical_not(is_hot)
    destination = home_row[group_ids]
    target = destination // own_groups
    local_row = (destination % own_groups).astype(jnp.float32)
    member = (
        (target[:, None] == jnp.arange(owners, dtype=jnp.int32)[None, :]) & keep[:, None]
    ).astype(jnp.int32)
    position = jnp.cumsum(member, axis=0) - 1
    placed = jnp.sum(position * member, axis=1)
    target_safe = jnp.where(keep, target, owners)
    placed_safe = jnp.where(keep, placed, 0)
    bucket = (
        jnp.zeros((owners, capacity, width), jnp.float32)
        .at[target_safe, placed_safe]
        .set(features, mode="drop")
    )
    labels = (
        jnp.full((owners, capacity), -1.0, jnp.float32)
        .at[target_safe, placed_safe]
        .set(local_row, mode="drop")
    )
    arrived, arrived_labels = sent_together((bucket, labels), OWNER, 0, 0, 2)
    total_rows = owners * capacity
    block = min(512, total_rows)
    flat_rows = arrived.reshape(total_rows // block, block, width)
    flat_labels = arrived_labels.astype(jnp.int32).reshape(total_rows // block, block)
    columns = jnp.arange(own_groups, dtype=jnp.int32)

    def add_block(carry, item):
        total, tally = carry
        block_rows, block_labels = item
        onehot = (block_labels[:, None] == columns[None, :]).astype(jnp.float32)
        total = total + lax.dot_general(
            onehot,
            block_rows,
            (((0,), (0,)), ((), ())),
            precision=lax.Precision.HIGHEST,
            preferred_element_type=jnp.float32,
        )
        tally = tally + jnp.sum(onehot, axis=0)
        return ((total, tally), None)

    start_carry = (
        jnp.zeros((own_groups, width), jnp.float32),
        jnp.zeros((own_groups,), jnp.float32),
    )
    (dense, dense_tally), _ = lax.scan(add_block, start_carry, (flat_rows, flat_labels))
    cold_sum, group_count = in_one_piece((dense, dense_tally), "rep", 0, 1)
    group_out = cold_sum / jnp.sqrt(1.0 + group_count)[:, None]
    return (group_out, group_count, hot_out, hot_count)


def solution(mesh):
    split = Mesh(
        mesh.devices.reshape(8, 4, 2, mesh.shape["rep"]), ("owner_0", "owner_1", "owner_2", "rep")
    )
    return jax.shard_map(
        local,
        mesh=split,
        in_specs=(P(OWNER_REP, None), P(OWNER_REP), P(OWNER_REP), P(), P()),
        out_specs=(P(OWNER_REP, None), P(OWNER_REP), P("rep", None), P("rep")),
        check_vma=False,
    )
```

profile of v0, /device:TPU:1, one launch (start us, length us, event | category | flops | bytes accessed | tf_op | source)
XLA Modules:
  0.0 193.5 jit_solution(14835666861502887366)
XLA Ops:
  0.7 0.7 compare_select_fusion.2
  1.4 0.9 compare_reduce_fusion
  2.3 3.1 %gather_fusion = s32[512]{0:T(512)S(1)} fusion(s32[65536]{0:T(1024)S(1)} %copy-done, s32[1024]{0:T(1024)S(1)} %pad_clamp_fusion), kind=kCustom, calls=%fused_computation | custom fusion | bytes 6144 | tf_op jit(solution)/shard_map/gather | solution.py:76
  5.6 1.2 reduce-window.6
  7.2 25.2 %scatter_fusion.1 = f32[64,16]{0,1:T(8,128)S(1)} fusion(f32[64,16]{0,1:T(8,128)S(1)} %broadcast_in_dim.53, s32[512]{0:T(512)S(1)} %bitcast.56, f32[512]{0:T(512)S(1)} %get-tuple-element.89), kind=kCustom, calls=%fused_computation.2 | custom fusion | bytes 10240 | tf_op jit(solution)/shard_map/scatter | solution.py:94
  32.4 0.3 copy.34
  32.9 0.6 copy-done.2
  33.4 26.3 %scatter_fusion = f32[64,16,256]{2,1,0:T(8,128)S(1)} fusion(f32[64,16,256]{2,1,0:T(8,128)S(1)} %broadcast_in_dim.48, s32[512]{0:T(512)S(1)} %bitcast.57, f32[512,256]{1,0:T(8,128)S(1)} %copy-done.2), kind=kCustom, calls=%fused_computation.1 | custom fusion | bytes 1576960 | tf_op jit(solution)/shard_map/scatter | solution.py:89
  59.8 1.3 pad_maximum_fusion
  61.0 14.9 %all-to-all-start = ((f32[64,16,257]{2,1,0:T(8,128)}), f32[64,16,257]{2,1,0:T(8,128)S(1)}, u32[]{:S(2)}, u32[]{:S(2)}) async-start(f32[64,16,257]{2,1,0:T(8,128)} %pad_maximum_fusion), calls=%async_computation | async-start | bytes 3145728 | tf_op jit(solution)/shard_map/all_to_all | solution.py:46
  76.0 0.8 select_reduce_fusion
  76.8 0.9 concatenate.35
  77.7 1.0 fusion.10
  78.7 0.8 pad_maximum_fusion.2
  79.4 35.6 %all-to-all-done = f32[64,16,257]{2,1,0:T(8,128)S(1)} async-done(((f32[64,16,257]{2,1,0:T(8,128)}), f32[64,16,257]{2,1,0:T(8,128)S(1)}, u32[]{:S(2)}, u32[]{:S(2)}) %all-to-all-start) | async-done | bytes 1052704 | tf_op jit(solution)/shard_map/all_to_all | solution.py:46
  115.1 6.8 %all-to-all-start.2 = ((f32[8,32,257]{2,1,0:T(8,128)}), f32[8,32,257]{2,1,0:T(8,128)}, u32[]{:S(2)}, u32[]{:S(2)}) async-start(f32[8,32,257]{2,1,0:T(8,128)} %pad_maximum_fusion.2), calls=%async_computation.2 | async-start | bytes 786432 | tf_op jit(solution)/shard_map/all_to_all | solution.py:20
  121.9 1.2 fusion.12
  123.1 1.3 split.9
  124.4 5.0 %while.13 = (s32[]{:T(128)}, f32[1024,256]{1,0:T(8,128)S(1)}, f32[1024]{0:T(1024)S(1)}, s32[2,512]{1,0:T(2,128)S(1)}, f32[2,512,256]{2,1,0:T(8,128)S(1)}, /*index=5*/s32[]{:T(128)}, s32[]{:T(128)}) while((s32[]{:T(128)}, f32[1024,256]{1,0:T(8,128)S(1)}, f32[1024]{0:T(1024)S(1)}, s32[2,512]{1,0:T(2,128)S(1)}, ...), condition=%wide.region_8.9_spmd.clone, body=%wide.region_6.0_spmd.clone.sunk | while | flops 1613235200 | bytes 2646120 | solution.py:121
  124.8 2.2 %fusion.36 = f32[1024,256]{1,0:T(8,128)S(1)} fusion(f32[1024,256]{1,0:T(8,128)S(1)} %get-tuple-element.129, s32[512]{0:T(512)S(1)} %bitcast.62, f32[2,512,256]{2,1,0:T(8,128)S(1)} %get-tuple-element.139, s32[]{:T(128)S(6)} %copy.46, pred[]{:T(512)S(6)} %compare.22), kind=kOutput, calls=%fused_computation.8.clone.1 | convolution fusion | flops 1611661312 | bytes 2623493 | tf_op jit(solution)/shard_map/while/body/eval_jaxpr/dot_general | solution.py:107
  126.9 0.3 fusion.37
  127.2 2.2 %fusion.36 = f32[1024,256]{1,0:T(8,128)S(1)} fusion(f32[1024,256]{1,0:T(8,128)S(1)} %get-tuple-element.129, s32[512]{0:T(512)S(1)} %bitcast.62, f32[2,512,256]{2,1,0:T(8,128)S(1)} %get-tuple-element.139, s32[]{:T(128)S(6)} %copy.46, pred[]{:T(512)S(6)} %compare.22), kind=kOutput, calls=%fused_computation.8.clone.1 | convolution fusion | flops 1611661312 | bytes 2623493 | tf_op jit(solution)/shard_map/while/body/eval_jaxpr/dot_general | solution.py:107
  129.8 1.5 copy.36
  131.2 3.3 %all-to-all-done.2 = f32[8,32,257]{2,1,0:T(8,128)} async-done(((f32[8,32,257]{2,1,0:T(8,128)}), f32[8,32,257]{2,1,0:T(8,128)}, u32[]{:S(2)}, u32[]{:S(2)}) %all-to-all-start.2) | async-done | bytes 263200 | tf_op jit(solution)/shard_map/all_to_all | solution.py:20
  134.5 3.6 %all-to-all-start.1 = ((f32[8,128,257]{1,2,0:T(8,128)}), f32[8,128,257]{1,2,0:T(8,128)S(1)}, u32[]{:S(2)}, u32[]{:S(2)}) async-start(f32[8,128,257]{1,2,0:T(8,128)} %copy.36), calls=%async_computation.1 | async-start | bytes 2162688 | tf_op jit(solution)/shard_map/all_to_all | solution.py:20
  138.1 1.0 reduce_sum.48
  139.2 26.8 %all-reduce = (f32[32,256]{1,0:T(8,128)S(1)}, f32[32]{0:T(128)S(1)}) all-reduce(f32[32,256]{1,0:T(8,128)S(1)} %slice.33, f32[32]{0:T(128)S(1)} %slice_reduce_fusion.1), channel_id=1, replica_groups=mesh['owner_0'=8,'owner_1'=4,'owner_2'=2,'rep'=8] {'owner_0'}, use_global_device_ids=true, to_apply=%region_12.13 | all-reduce | flops 8224 | bytes 65792 | tf_op jit(solution)/shard_map/psum | solution.py:37
  166.0 11.9 %all-reduce.1 = (f32[32,256]{1,0:T(8,128)S(1)}, f32[32]{0:T(128)S(1)}) all-reduce(f32[32,256]{1,0:T(8,128)S(1)} %get-tuple-element.77, f32[32]{0:T(128)S(1)} %get-tuple-element.78), channel_id=1, replica_groups=mesh['owner_0'=8,'owner_1'=4,'owner_2'=2,'rep'=8] {'owner_1'}, use_global_device_ids=true, to_apply=%region_13.14 | all-reduce | flops 8224 | bytes 65792 | tf_op jit(solution)/shard_map/psum | solution.py:37
  177.9 13.6 %all-reduce.2 = (f32[32,256]{1,0:T(8,128)S(1)}, f32[32]{0:T(128)S(1)}) all-reduce(f32[32,256]{1,0:T(8,128)S(1)} %get-tuple-element.79, f32[32]{0:T(128)S(1)} %get-tuple-element.80), channel_id=1, replica_groups=mesh['owner_0'=8,'owner_1'=4,'owner_2'=2,'rep'=8] {'owner_2'}, use_global_device_ids=true, to_apply=%region_14.15 | all-reduce | flops 8224 | bytes 65792 | tf_op jit(solution)/shard_map/psum | solution.py:37
  191.5 0.7 broadcast_divide_fusion
  192.2 0.5 slice_bitcast_fusion
  192.8 0.8 copy.38
  (41 shorter events, 1.6 us)
Async XLA Ops:
  0.6 1.7 copy-start
  0.6 4.9 %copy-start.5 = (s32[512]{0:T(512)S(1)}, s32[512]{0:T(512)}, u32[]{:S(2)}) copy-start(s32[512]{0:T(512)} %param.9) | copy-start | bytes 6148
  32.4 1.0 copy-start.2
  61.0 15.0 %copy-start.3 = (s32[512]{0:T(512)S(1)}, s32[512]{0:T(512)}, u32[]{:S(2)}) copy-start(s32[512]{0:T(512)} %param.8) | copy-start | bytes 6148
  61.0 15.0 %copy-start.4 = (s32[256]{0:T(256)S(1)}, s32[256]{0:T(256)}, u32[]{:S(2)}) copy-start(s32[256]{0:T(256)} %param.11) | copy-start | bytes 3076
  61.0 54.0 %all-to-all-start = ((f32[64,16,257]{2,1,0:T(8,128)}), f32[64,16,257]{2,1,0:T(8,128)S(1)}, u32[]{:S(2)}, u32[]{:S(2)}) async-start(f32[64,16,257]{2,1,0:T(8,128)} %pad_maximum_fusion), calls=%async_computation | async-start | bytes 3145728 | tf_op jit(solution)/shard_map/all_to_all | solution.py:46
  115.1 8.0 %copy-start.1 = (f32[64,16,257]{2,1,0:T(8,128)}, f32[64,16,257]{2,1,0:T(8,128)S(1)}, u32[]{:S(2)}) copy-start(f32[64,16,257]{2,1,0:T(8,128)S(1)} %all-to-all-done) | copy-start | bytes 3158020
  115.1 19.5 %all-to-all-start.2 = ((f32[8,32,257]{2,1,0:T(8,128)}), f32[8,32,257]{2,1,0:T(8,128)}, u32[]{:S(2)}, u32[]{:S(2)}) async-start(f32[8,32,257]{2,1,0:T(8,128)} %pad_maximum_fusion.2), calls=%async_computation.2 | async-start | bytes 786432 | tf_op jit(solution)/shard_map/all_to_all | solution.py:20
  134.5 57.7 %all-to-all-start.1 = ((f32[8,128,257]{1,2,0:T(8,128)}), f32[8,128,257]{1,2,0:T(8,128)S(1)}, u32[]{:S(2)}, u32[]{:S(2)}) async-start(f32[8,128,257]{1,2,0:T(8,128)} %copy.36), calls=%async_computation.1 | async-start | bytes 2162688 | tf_op jit(solution)/shard_map/all_to_all | solution.py:20
  191.4 2.1 %copy-start.6 = (f32[32]{0:T(128)}, f32[32]{0:T(128)S(1)}, u32[]{:S(2)}) copy-start(f32[32]{0:T(128)S(1)} %get-tuple-element.82) | copy-start | bytes 388
where the time goes:
time: 194 us
  local copies, waits for them, and re-layouts  60.8 us (31%)
  blocking collectives  52.2 us (27%)
  waiting for transfers between devices  38.9 us (20%)
  starting transfers between devices  25.3 us (13%)
  other arithmetic  10.1 us (5%)
  matrix products  5.27 us (3%)
    psum x3, blocking collectives, one_axis_at_a_time(): shard = lax.psum(shard, axis)  52.2 us
    all_to_all x1, waiting for transfers between devices, sent_together(): lax.all_to_all(both, axis, split_axis=split_dim, concat_axis=concat_dim,...  35.6 us
    scatter x1, local copies, waits for them, and re-layouts, local(): bucket = jnp.zeros((owners, capacity, width), jnp.float32).at[target_safe...  26.3 us
    scatter x1, local copies, waits for them, and re-layouts, local(): labels = jnp.full((owners, capacity), -1.0, jnp.float32).at[target_safe,...  25.2 us
    all_to_all x1, starting transfers between devices, sent_together(): lax.all_to_all(both, axis, split_axis=split_dim, concat_axis=concat_dim,...  14.9 us
    all_to_all x2, starting transfers between devices, sent_and_summed(): lax.all_to_all(split_up(shard, dim, devices), axis, 0, 0, tiled=True)  10.4 us
    dot_general x2, matrix products, add_block(): lax.dot_general(onehot, block_rows, (((0,), (0,)), ((), ())), precision=l...  4.31 us
  transfers between devices with their start and end apart: 3, of which 2 were waited for; matrix products, arithmetic and copies ran while one was open for 7% of the time, Pallas kernels for 0%

commit v1 on v0

v1 whole, which is shorter than its diff:
```python
import functools

import jax
import jax.numpy as jnp
from jax import lax
from jax.experimental import pallas as pl
from jax.experimental.pallas import tpu as pltpu
from jax.sharding import PartitionSpec as P

OWNER_REP = ("owner", "rep")
MESH = pl.DeviceIdType.MESH
LANES = 128
CAP = 16
INNER = 8


def iota(shape, dim):
    return lax.broadcasted_iota(jnp.int32, shape, dim)


def ones_where(mask):
    return jnp.where(mask, 1.0, 0.0)


def two_parts(x):
    high = x.astype(jnp.bfloat16)
    low = (x - high.astype(jnp.float32)).astype(jnp.bfloat16)
    return high, low


def dot(a, b, dims=(((1,), (0,)), ((), ()))):
    return lax.dot_general(a, b, dims, preferred_element_type=jnp.float32)


def folded(x):
    return x[:, :LANES] + x[:, LANES:]


def column(row):
    n = row.shape[1]
    square = jnp.where(iota((n, n), 0) == iota((n, n), 1), row, 0.0)
    return jnp.sum(square, axis=1, keepdims=True)


def diagonal(square):
    n = square.shape[0]
    return jnp.sum(
        jnp.where(iota((n, n), 0) == iota((n, n), 1), square, 0.0), axis=0, keepdims=True
    )


def kernel(
    sizes,
    gid_ref,
    live_ref,
    hot_ref,
    feat_hbm,
    home_hbm,
    gout,
    gcount,
    hout,
    hcount,
    feat,
    home,
    parts,
    bucket,
    rbucket,
    label,
    rlabel,
    wide,
    rhs,
    dense,
    rdense,
    count,
    rcount,
    hpart,
    rhpart,
    hnum,
    rhnum,
    piece,
    rpiece,
    done,
    rdone,
    in_sem,
    send,
    recv,
):
    n_own, n_rep, own_groups, n_hot = sizes
    rows = gid_ref.shape[1]
    per_rep = own_groups // n_rep
    hot_rep = n_hot // n_rep
    n_z = n_own // INNER
    me = lax.axis_index("owner")
    my = lax.axis_index("rep")

    def peer(i):
        m, k = i // n_z, i % n_z
        dz = ((k + 1) // 2) * (1 - 2 * (k % 2))
        z = (me // INNER + dz + n_z) % n_z
        x = ((me % INNER) // 2 + m // 2) % (INNER // 2)
        return z * INNER + x * 2 + (me + m) % 2

    def rep_peer(i):
        step = (i // 2 + 1) * (1 - 2 * (i % 2))
        return (my + step + n_rep) % n_rep

    barrier = pltpu.get_barrier_semaphore()

    @pl.loop(1, n_own)
    def _(i):
        pl.semaphore_signal(barrier, inc=1, device_id=(peer(i), my), device_id_type=MESH)

    @pl.loop(0, n_rep - 1)
    def _(i):
        pl.semaphore_signal(barrier, inc=1, device_id=(me, rep_peer(i)), device_id_type=MESH)

    get_home = pltpu.make_async_copy(home_hbm, home, in_sem.at[0])
    get_feat = pltpu.make_async_copy(feat_hbm, feat, in_sem.at[1])
    get_home.start()
    get_feat.start()

    gid = gid_ref[...]
    live = live_ref[...] == 1
    match = iota((n_hot, n_hot), 0) == iota((n_hot, n_hot), 1)
    hot_ids = jnp.sum(
        jnp.where(match, hot_ref[...].astype(jnp.float32), 0.0), axis=1, keepdims=True
    )
    hits = ones_where(hot_ids == gid.astype(jnp.float32))
    is_hot = jnp.max(hits, axis=0, keepdims=True) > 0.5
    hot_table = jnp.where(live, hits, 0.0).astype(jnp.bfloat16)
    keep = jnp.logical_and(live, jnp.logical_not(is_hot))

    get_home.wait()
    n_hi = home.shape[0]
    digits = jnp.concatenate(
        [
            (home[...] >> 8).astype(jnp.float32).astype(jnp.bfloat16),
            (home[...] & 255).astype(jnp.float32).astype(jnp.bfloat16),
        ],
        axis=1,
    )
    pick = ones_where(iota((n_hi, rows), 0) == (gid >> 7)).astype(jnp.bfloat16)
    found = dot(digits, pick, (((0,), (0,)), ((), ())))
    low = iota((LANES, rows), 0) == (gid & 127)
    d_high = jnp.sum(jnp.where(low, found[:LANES], 0.0), axis=0, keepdims=True)
    d_low = jnp.sum(jnp.where(low, found[LANES:], 0.0), axis=0, keepdims=True)
    dest = (d_high * 256.0 + d_low).astype(jnp.int32)
    owner = dest // own_groups
    local = dest % own_groups + 1
    member = ones_where(jnp.logical_and(iota((n_own, rows), 0) == owner, keep))
    before = ones_where(iota((rows, rows), 0) < iota((rows, rows), 1)).astype(jnp.bfloat16)
    earlier = dot(member.astype(jnp.bfloat16), before)
    pos = jnp.sum(member * earlier, axis=0, keepdims=True).astype(jnp.int32)
    slot = jnp.where(keep, owner * CAP + pos, -1)

    shift = (me % (LANES // CAP)) * CAP
    at = ones_where(iota((LANES, rows), 0) == pos + shift).astype(jnp.bfloat16)
    two = jnp.concatenate(
        [member * (local >> 5).astype(jnp.float32), member * (local & 31).astype(jnp.float32)],
        axis=0,
    ).astype(jnp.bfloat16)
    two = dot(two, at, (((1,), (1,)), ((), ())))
    names = (two[:n_own] * 32.0 + two[n_own:]).astype(jnp.int32)
    label[...] = names.reshape(n_own, 1, LANES)

    get_feat.wait()
    for h in range(2):
        high, lo = two_parts(feat[:, h * LANES : (h + 1) * LANES])
        parts[h, :, :LANES] = high
        parts[h, :, LANES:] = lo

    def pack(h):
        per = LANES // CAP

        @pl.loop(0, n_own // per)
        def _(j):
            chosen = ones_where(iota((LANES, rows), 0) + j * LANES == slot).astype(jnp.bfloat16)
            packed = folded(dot(chosen, parts[h]))
            bucket[h, pl.ds(j * per, per)] = packed.reshape(per, CAP, LANES)

    pack(0)
    for h in range(2):
        part = folded(dot(hot_table, parts[h]))
        hpart[:, :, h * LANES : (h + 1) * LANES] = part.reshape(n_rep, hot_rep, LANES)
    tally = dot(hot_table, jnp.ones((rows, n_hot), jnp.bfloat16))
    hnum[...] = diagonal(tally)

    rlabel[me] = label[me]
    rbucket[0, me] = bucket[0, me]
    rhpart[my] = hpart[my]
    rhnum[my] = hnum[...]

    pl.semaphore_wait(barrier, n_own - 1 + n_rep - 1)

    def to_owner(src, dst, which, i_peer):
        pltpu.make_async_remote_copy(
            src_ref=src,
            dst_ref=dst,
            send_sem=send.at[which],
            recv_sem=recv.at[which],
            device_id=(i_peer, my),
            device_id_type=MESH,
        ).start()

    def to_rep(src, dst, which, i_peer):
        pltpu.make_async_remote_copy(
            src_ref=src,
            dst_ref=dst,
            send_sem=send.at[which],
            recv_sem=recv.at[which],
            device_id=(me, i_peer),
            device_id_type=MESH,
        ).start()

    def arrived(ref, which, n):
        pltpu.make_async_copy(ref.at[pl.ds(0, n)], ref.at[pl.ds(0, n)], recv.at[which]).wait()

    def left(ref, which, n):
        pltpu.make_async_copy(ref.at[pl.ds(0, n)], ref.at[pl.ds(0, n)], send.at[which]).wait()

    @pl.loop(0, n_rep - 1)
    def _(i):
        o = rep_peer(i)
        to_rep(hpart.at[o], rhpart.at[my], 0, o)
        to_rep(hnum, rhnum.at[my], 1, o)

    @pl.loop(1, n_own)
    def _(i):
        o = peer(i)
        to_owner(label.at[o], rlabel.at[me], 2, o)
        to_owner(bucket.at[0, o], rbucket.at[0, me], 3, o)

    pack(1)
    rbucket[1, me] = bucket[1, me]

    arrived(rhpart, 0, n_rep - 1)
    arrived(rhnum, 1, n_rep - 1)
    hsum = jnp.sum(rhpart[...], axis=0)
    num = jnp.sum(rhnum[...], axis=0)
    mine = iota((hot_rep, n_hot), 1) == iota((hot_rep, n_hot), 0) + my * hot_rep
    num = jnp.sum(jnp.where(mine, num, 0.0), axis=1, keepdims=True)
    num = jnp.broadcast_to(num, (hot_rep, LANES)).reshape(hot_rep, 1, LANES)
    for h in range(2):
        block = hsum[:, h * LANES : (h + 1) * LANES].reshape(hot_rep, 1, LANES)
        piece[h * hot_rep : (h + 1) * hot_rep, :, :LANES] = block
        piece[h * hot_rep : (h + 1) * hot_rep, :, LANES:] = num
    rpiece[me] = piece[me]

    @pl.loop(1, n_own)
    def _(i):
        o = peer(i)
        to_owner(piece.at[o], rpiece.at[me], 4, o)

    @pl.loop(1, n_own)
    def _(i):
        o = peer(i)
        to_owner(bucket.at[1, o], rbucket.at[1, me], 5, o)

    arrived(rlabel, 2, n_own - 1)
    per = LANES // CAP
    for j in range(n_own // per):
        wide[:, j * LANES : (j + 1) * LANES] = jnp.sum(rlabel[j * per : (j + 1) * per], axis=0)

    def add_up(h):
        high, lo = two_parts(rbucket[h].reshape(n_own * CAP, LANES))
        rhs[:, :LANES] = high
        rhs[:, LANES:] = lo

        def block(b):
            names = iota((per_rep, n_own * CAP), 0) + b * per_rep + 1
            hit = ones_where(names == wide[...]).astype(jnp.bfloat16)
            if h == 0:
                tally = dot(hit, jnp.ones((n_own * CAP, per_rep), jnp.bfloat16))
                return folded(dot(hit, rhs[...])), diagonal(tally)
            return folded(dot(hit, rhs[...])), None

        @pl.loop(0, n_rep - 1)
        def _(i):
            b = rep_peer(i)
            sums, tally = block(b)
            dense[h, b] = sums
            if h == 0:
                count[b] = tally

            @pl.when(i > 0)
            def _():
                o = rep_peer(i - 1)
                to_rep(dense.at[h, o], rdense.at[h, my], 6 + 2 * h, o)

        sums, tally = block(my)
        rdense[h, my] = sums
        if h == 0:
            rcount[my] = tally
        o = rep_peer(n_rep - 2)
        to_rep(dense.at[h, o], rdense.at[h, my], 6 + 2 * h, o)
        if h == 0:

            @pl.loop(0, n_rep - 1)
            def _(i):
                o = rep_peer(i)
                to_rep(count.at[o], rcount.at[my], 7, o)

    arrived(rbucket.at[0], 3, n_own - 1)
    add_up(0)

    arrived(rpiece, 4, n_own - 1)
    total = jnp.sum(rpiece[...], axis=0)
    done[:, :LANES] = total[:, :LANES] / jnp.sqrt(1.0 + total[:, LANES:])
    done[:, LANES:] = total[:, LANES:]
    rdone[me] = done[...]

    @pl.loop(1, n_own)
    def _(i):
        to_owner(done, rdone.at[me], 9, peer(i))

    arrived(rbucket.at[1], 5, n_own - 1)
    add_up(1)

    arrived(rdone, 9, n_own - 1)
    for h in range(2):
        block = rdone[h * hot_rep : (h + 1) * hot_rep, :, :LANES]
        hout[:, h * LANES : (h + 1) * LANES] = block.reshape(hot_rep, LANES)
    tally = rdone[:hot_rep, :, LANES : LANES + hot_rep].reshape(hot_rep, hot_rep)
    hcount[...] = diagonal(tally)

    arrived(rcount, 7, n_rep - 1)
    num = jnp.sum(rcount[...], axis=0)
    gcount[...] = num
    root = jnp.sqrt(1.0 + column(num))
    for h in range(2):
        arrived(rdense.at[h], 6 + 2 * h, n_rep - 1)
        gout[:, h * LANES : (h + 1) * LANES] = jnp.sum(rdense[h], axis=0) / root

    left(rhpart, 0, n_rep - 1)
    left(rhnum, 1, n_rep - 1)
    left(rlabel, 2, n_own - 1)
    left(rbucket.at[0], 3, n_own - 1)
    left(rpiece, 4, n_own - 1)
    left(rbucket.at[1], 5, n_own - 1)
    left(rdense.at[0], 6, n_rep - 1)
    left(rcount, 7, n_rep - 1)
    left(rdense.at[1], 8, n_rep - 1)
    left(rdone, 9, n_own - 1)


def local(n_own, n_rep, features, group_ids, survive, home_row, hot_ids):
    rows, width = features.shape
    groups, n_hot = home_row.shape[0], hot_ids.shape[0]
    own_groups = groups // n_own
    per_rep, hot_rep = own_groups // n_rep, n_hot // n_rep
    f32, i32 = jnp.float32, jnp.int32
    vmem = pl.BlockSpec(memory_space=pltpu.VMEM)
    hbm = pl.BlockSpec(memory_space=pl.ANY)
    gout, gcount, hout, hcount = pl.pallas_call(
        functools.partial(kernel, (n_own, n_rep, own_groups, n_hot)),
        out_shape=(
            jax.ShapeDtypeStruct((per_rep, width), f32),
            jax.ShapeDtypeStruct((1, per_rep), f32),
            jax.ShapeDtypeStruct((hot_rep, width), f32),
            jax.ShapeDtypeStruct((1, hot_rep), f32),
        ),
        in_specs=[vmem, vmem, vmem, hbm, hbm],
        out_specs=(vmem, vmem, vmem, vmem),
        scratch_shapes=[
            pltpu.VMEM((rows, width), f32),
            pltpu.VMEM((groups // LANES, LANES), i32),
            pltpu.VMEM((2, rows, 2 * LANES), jnp.bfloat16),
            pltpu.VMEM((2, n_own, CAP, LANES), f32),
            pltpu.VMEM((2, n_own, CAP, LANES), f32),
            pltpu.VMEM((n_own, 1, LANES), i32),
            pltpu.VMEM((n_own, 1, LANES), i32),
            pltpu.VMEM((1, n_own * CAP), i32),
            pltpu.VMEM((n_own * CAP, 2 * LANES), jnp.bfloat16),
            pltpu.VMEM((2, n_rep, per_rep, LANES), f32),
            pltpu.VMEM((2, n_rep, per_rep, LANES), f32),
            pltpu.VMEM((n_rep, 1, per_rep), f32),
            pltpu.VMEM((n_rep, 1, per_rep), f32),
            pltpu.VMEM((n_rep, hot_rep, width), f32),
            pltpu.VMEM((n_rep, hot_rep, width), f32),
            pltpu.VMEM((1, n_hot), f32),
            pltpu.VMEM((n_rep, 1, n_hot), f32),
            pltpu.VMEM((n_own, 1, 2 * LANES), f32),
            pltpu.VMEM((n_own, 1, 2 * LANES), f32),
            pltpu.VMEM((1, 2 * LANES), f32),
            pltpu.VMEM((n_own, 1, 2 * LANES), f32),
            pltpu.SemaphoreType.DMA((2,)),
            pltpu.SemaphoreType.DMA((10,)),
            pltpu.SemaphoreType.DMA((10,)),
        ],
        compiler_params=pltpu.CompilerParams(
            collective_id=0, has_side_effects=True, vmem_limit_bytes=32 * 1024 * 1024
        ),
    )(
        group_ids.reshape(1, rows),
        survive.reshape(1, rows),
        hot_ids.reshape(1, n_hot),
        features,
        home_row.reshape(groups // LANES, LANES),
    )
    return gout, gcount.reshape(per_rep), hout, hcount.reshape(hot_rep)


def solution(mesh):
    return jax.shard_map(
        functools.partial(local, mesh.shape["owner"], mesh.shape["rep"]),
        mesh=mesh,
        in_specs=(P(OWNER_REP, None), P(OWNER_REP), P(OWNER_REP), P(), P()),
        out_specs=(P(OWNER_REP, None), P(OWNER_REP), P("rep", None), P("rep")),
        check_vma=False,
    )
```

time: 194 us -> 68.1 us (0.35)
  Pallas kernels: 0 us -> 61.2 us
  local copies, waits for them, and re-layouts: 60.8 us -> 4.97 us
  blocking collectives: 52.2 us -> 0 us
  waiting for transfers between devices: 38.9 us -> 0 us
  starting transfers between devices: 25.3 us -> 0 us
  other arithmetic: 10.1 us -> 0 us
  matrix products: 5.27 us -> 0 us
    pallas_call x0 -> x1, Pallas kernels: none -> 61.2 us  [local(): pl.pallas_call(functools.partial(kernel, (n_own, n_rep, own_groups, n_hot...]
    psum x3 -> x0, blocking collectives: 52.2 us -> none  [one_axis_at_a_time(): shard = lax.psum(shard, axis)]
    scatter x2 -> x0, local copies, waits for them, and re-layouts: 51.5 us -> none  [the longest x1 26.3 us: local(): bucket = jnp.zeros((owners, capacity, width), jnp.float32).at[target_safe...]
    all_to_all x3 -> x0, waiting for transfers between devices: 38.9 us -> none  [the longest x1 35.6 us: sent_together(): lax.all_to_all(both, axis, split_axis=split_dim, concat_axis=concat_dim,...]
    all_to_all x3 -> x0, starting transfers between devices: 25.3 us -> none  [the longest x1 14.9 us: sent_together(): lax.all_to_all(both, axis, split_axis=split_dim, concat_axis=concat_dim,...]
    dot_general x3 -> x0, matrix products: 5.27 us -> none  [the longest x2 4.31 us: add_block(): lax.dot_general(onehot, block_rows, (((0,), (0,)), ((), ())), precision=l...]
    unnamed x15 -> x14, local copies, waits for them, and re-layouts: 1.38 us -> 4.97 us
    gather x1 -> x0, local copies, waits for them, and re-layouts: 3.14 us -> none  [local(): destination = home_row[group_ids]]
  transfers between devices with their start and end apart: 3 -> 0, of which waited for: 2 -> 0; matrix products, arithmetic and copies ran while one was open for 7% -> 0% of each run, Pallas kernels for 0% -> 0%
where the time goes in v1:
time: 68.1 us; the launch traced here: 66.8 us
  Pallas kernels  61.2 us (90%)
  local copies, waits for them, and re-layouts  4.97 us (7%)
    pallas_call x1, Pallas kernels, local(): pl.pallas_call(functools.partial(kernel, (n_own, n_rep, own_groups, n_hot...  61.2 us
    unnamed x14, local copies, waits for them, and re-layouts  4.97 us

profile of v1, /device:TPU:1, one launch (start us, length us, event | category | flops | bytes accessed | tf_op | source)
XLA Modules:
  0.0 66.8 jit_solution(8049285775525983926)
XLA Ops:
  0.6 0.0 copy-start.3
  0.6 0.0 copy-start.2
  0.7 0.0 copy-start.4
  0.7 0.7 copy-done.3
  1.3 0.0 copy-done.2
  1.3 0.0 copy-done.4
  1.3 0.0 copy-start
  1.3 1.0 %copy-done = f32[512,256]{1,0:T(8,128)S(1)} copy-done((f32[512,256]{1,0:T(8,128)S(1)}, f32[512,256]{1,0:T(8,128)}, u32[]{:S(2)}) %copy-start) | copy-done | bytes 524312
  2.4 0.0 copy-start.1
  2.4 0.9 %copy-done.1 = s32[65536]{0:T(1024)S(1)} copy-done((s32[65536]{0:T(1024)S(1)}, s32[65536]{0:T(1024)}, u32[]{:S(2)}) %copy-start.1) | copy-done | bytes 262168
  3.3 61.2 %shard_map.84 = (f32[128,256]{1,0:T(8,128)S(1)}, f32[1,128]{1,0:T(1,128)S(1)}, f32[32,256]{1,0:T(8,128)S(1)}, f32[1,32]{1,0:T(1,128)S(1)}) custom-call(s32[1,512]{1,0:T(1,128)S(1)} %bitcast.7, s32[1,512]{1,0:T(1,128)S(1)} %bitcast.8, s32[1,256]{1,0:T(1,128)S(1)} %bitcast.9, f32[512,256]{1,0:T(8,128)S(1)} %copy-done, s32[512,128]{1,0:T(8,128)S(1)} %bitcast.6), custom_call_target="tpu_custom_call" | custom-call | tf_op jit(solution)/shard_map/pallas_call | solution.py:354
  64.5 0.7 copy.13
  65.2 0.5 copy.14
  65.7 0.6 copy.15
  66.3 0.5 copy.16
Async XLA Ops:
  0.6 0.7 %copy-start.3 = (s32[512]{0:T(512)S(1)}, s32[512]{0:T(512)}, u32[]{:S(2)}) copy-start(s32[512]{0:T(512)} %param.7) | copy-start | bytes 6148
  0.6 0.7 %copy-start.2 = (s32[512]{0:T(512)S(1)}, s32[512]{0:T(512)}, u32[]{:S(2)}) copy-start(s32[512]{0:T(512)} %param.6) | copy-start | bytes 6148
  0.7 0.7 %copy-start.4 = (s32[256]{0:T(256)S(1)}, s32[256]{0:T(256)}, u32[]{:S(2)}) copy-start(s32[256]{0:T(256)} %param.9) | copy-start | bytes 3076
  1.3 1.0 %copy-start = (f32[512,256]{1,0:T(8,128)S(1)}, f32[512,256]{1,0:T(8,128)}, u32[]{:S(2)}) copy-start(f32[512,256]{1,0:T(8,128)} %feat_hbm.1) | copy-start | bytes 1572868
  2.4 0.9 %copy-start.1 = (s32[65536]{0:T(1024)S(1)}, s32[65536]{0:T(1024)}, u32[]{:S(2)}) copy-start(s32[65536]{0:T(1024)} %param.8) | copy-start | bytes 786436

commit v2 on v1

v2 whole, which is shorter than its diff:
```python
import functools

import jax
import jax.numpy as jnp
from jax import lax
from jax.experimental import pallas as pl
from jax.experimental.pallas import tpu as pltpu
from jax.sharding import PartitionSpec as P

OWNER_REP = ("owner", "rep")
MESH = pl.DeviceIdType.MESH
LANES = 128
HALF = 64
CAP = 16
DEEP = 8
INNER = 8


def iota(shape, dim):
    return lax.broadcasted_iota(jnp.int32, shape, dim)


def ones_where(mask):
    return jnp.where(mask, 1.0, 0.0)


def two_parts(x):
    high = x.astype(jnp.bfloat16)
    low = (x - high.astype(jnp.float32)).astype(jnp.bfloat16)
    return high, low


def dot(a, b, dims=(((1,), (0,)), ((), ()))):
    return lax.dot_general(a, b, dims, preferred_element_type=jnp.float32)


def folded(x):
    return x[:, :LANES] + x[:, LANES:]


def column(row):
    n = row.shape[1]
    square = jnp.where(iota((n, n), 0) == iota((n, n), 1), row, 0.0)
    return jnp.sum(square, axis=1, keepdims=True)


def diagonal(square):
    n = square.shape[0]
    return jnp.sum(
        jnp.where(iota((n, n), 0) == iota((n, n), 1), square, 0.0), axis=0, keepdims=True
    )


def left_half(a, b):
    return jnp.where(iota(a.shape, 1) < HALF, a, b)


def turned(x):
    return pltpu.roll(x, HALF, 1)


def kernel(
    sizes,
    gid_hbm,
    live_hbm,
    hot_hbm,
    feat_hbm,
    home_hbm,
    gout,
    gcount,
    hout,
    hcount,
    gid_ref,
    live_ref,
    hot_ref,
    feat,
    home,
    parts,
    bucket,
    rbucket,
    label,
    rlabel,
    hits_of,
    rhs,
    dense,
    rdense,
    count,
    rcount,
    hpart,
    rhpart,
    hnum,
    rhnum,
    piece,
    rpiece,
    done,
    rdone,
    in_sem,
    send,
    recv,
):
    n_own, n_rep, own_groups, n_hot = sizes
    rows = gid_ref.shape[1]
    per_rep = own_groups // n_rep
    hot_rep = n_hot // n_rep
    n_z = n_own // INNER
    slots = n_own * DEEP
    me = lax.axis_index("owner")
    my = lax.axis_index("rep")
    zs = []
    for k in range(n_z):
        dz = ((k + 1) // 2) * (1 - 2 * (k % 2))
        zs.append(lax.rem(lax.div(me, INNER) + (dz + n_z), n_z) * INNER)
    x_me, c_me = lax.div(lax.rem(me, INNER), 2), lax.rem(me, 2)

    def each_owner(act):
        @pl.loop(0, INNER)
        def _(m):
            inner = lax.rem(x_me + lax.div(m, 2), INNER // 2) * 2 + lax.rem(c_me + m, 2)
            for k in range(n_z):
                if k == 0:

                    @pl.when(m > 0)
                    def _():
                        act(zs[0] + inner)
                else:
                    act(zs[k] + inner)

    def rep_at(step):
        return lax.rem(my + (step + n_rep), n_rep)

    copies = []
    for i, (src, dst) in enumerate(
        [
            (home_hbm, home),
            (gid_hbm, gid_ref),
            (live_hbm, live_ref),
            (hot_hbm, hot_ref),
            (feat_hbm, feat),
        ]
    ):
        copies.append(pltpu.make_async_copy(src, dst, in_sem.at[i]))
        copies[-1].start()

    barrier = pltpu.get_barrier_semaphore()

    def greet(o):
        pl.semaphore_signal(barrier, inc=1, device_id=(o, my), device_id_type=MESH)

    each_owner(greet)
    for step in range(1, n_rep):
        pl.semaphore_signal(barrier, inc=1, device_id=(me, rep_at(step)), device_id_type=MESH)

    for copy in copies[:4]:
        copy.wait()

    gid = gid_ref[...]
    live = live_ref[...] == 1
    match = iota((n_hot, n_hot), 0) == iota((n_hot, n_hot), 1)
    hot_ids = jnp.sum(
        jnp.where(match, hot_ref[...].astype(jnp.float32), 0.0), axis=1, keepdims=True
    )
    hits = ones_where(hot_ids == gid.astype(jnp.float32))
    is_hot = jnp.max(hits, axis=0, keepdims=True) > 0.5
    hot_table = jnp.where(live, hits, 0.0).astype(jnp.bfloat16)
    keep = jnp.logical_and(live, jnp.logical_not(is_hot))

    n_hi = home.shape[0]
    digits = jnp.concatenate(
        [
            (home[...] >> 8).astype(jnp.float32).astype(jnp.bfloat16),
            (home[...] & 255).astype(jnp.float32).astype(jnp.bfloat16),
        ],
        axis=1,
    )
    pick = ones_where(iota((n_hi, rows), 0) == (gid >> 7)).astype(jnp.bfloat16)
    found = dot(digits, pick, (((0,), (0,)), ((), ())))
    low = iota((LANES, rows), 0) == (gid & 127)
    d_high = jnp.sum(jnp.where(low, found[:LANES], 0.0), axis=0, keepdims=True)
    d_low = jnp.sum(jnp.where(low, found[LANES:], 0.0), axis=0, keepdims=True)
    dest = (d_high * 256.0 + d_low).astype(jnp.int32)
    owner = dest // own_groups
    local = dest % own_groups + 1
    member = ones_where(jnp.logical_and(iota((n_own, rows), 0) == owner, keep))
    before = ones_where(iota((rows, rows), 0) < iota((rows, rows), 1)).astype(jnp.bfloat16)
    earlier = dot(member.astype(jnp.bfloat16), before)
    pos = jnp.sum(member * earlier, axis=0, keepdims=True).astype(jnp.int32)
    deep = pos >= DEEP
    slot_a = jnp.where(jnp.logical_and(keep, jnp.logical_not(deep)), owner * DEEP + pos, -1)
    slot_b = jnp.where(jnp.logical_and(keep, deep), owner * DEEP + pos - DEEP, -1)

    shift = lax.rem(me, HALF // DEEP) * DEEP
    place = jnp.where(deep, pos + (HALF - DEEP), pos) + shift
    at = ones_where(iota((LANES, rows), 0) == place).astype(jnp.bfloat16)
    two = jnp.concatenate(
        [member * (local >> 5).astype(jnp.float32), member * (local & 31).astype(jnp.float32)],
        axis=0,
    ).astype(jnp.bfloat16)
    two = dot(two, at, (((1,), (1,)), ((), ())))
    names = (two[:n_own] * 32.0 + two[n_own:]).astype(jnp.int32)
    label[...] = names.reshape(n_own, 1, LANES)
    rlabel[me] = label[me]

    copies[4].wait()
    for t in range(2):
        block = feat[:, t * LANES : (t + 1) * LANES]
        for v in range(2):
            high, lo = two_parts(turned(block) if v else block)
            parts[t, v, :, :LANES] = high
            parts[t, v, :, LANES:] = lo

    tall = min(256, slots)

    def pack(t):
        @pl.loop(0, slots // tall)
        def _(j):
            lines = iota((tall, rows), 0) + j * tall
            a = folded(dot(ones_where(lines == slot_a).astype(jnp.bfloat16), parts[t, 0]))
            b = folded(dot(ones_where(lines == slot_b).astype(jnp.bfloat16), parts[t, 1]))
            to = pl.ds(j * (tall // DEEP), tall // DEEP)
            bucket[2 * t, to] = left_half(a, b).reshape(tall // DEEP, DEEP, LANES)
            bucket[2 * t + 1, to] = left_half(b, a).reshape(tall // DEEP, DEEP, LANES)

        for c in (2 * t, 2 * t + 1):
            rbucket[c, me] = bucket[c, me]

    def to_owner(src, dst, which, o):
        pltpu.make_async_remote_copy(
            src_ref=src,
            dst_ref=dst,
            send_sem=send.at[which],
            recv_sem=recv.at[which],
            device_id=(o, my),
            device_id_type=MESH,
        ).start()

    def to_rep(src, dst, which, o):
        pltpu.make_async_remote_copy(
            src_ref=src,
            dst_ref=dst,
            send_sem=send.at[which],
            recv_sem=recv.at[which],
            device_id=(me, o),
            device_id_type=MESH,
        ).start()

    def arrived(ref, which, n):
        pltpu.make_async_copy(ref.at[pl.ds(0, n)], ref.at[pl.ds(0, n)], recv.at[which]).wait()

    def left(ref, which, n):
        pltpu.make_async_copy(ref.at[pl.ds(0, n)], ref.at[pl.ds(0, n)], send.at[which]).wait()

    pack(0)
    pl.semaphore_wait(barrier, n_own - 1 + n_rep - 1)

    def send_first(o):
        to_owner(label.at[o], rlabel.at[me], 2, o)
        to_owner(bucket.at[0, o], rbucket.at[0, me], 3, o)

    each_owner(send_first)

    for t in range(2):
        part = folded(dot(hot_table, parts[t, 0]))
        hpart[:, :, t * LANES : (t + 1) * LANES] = part.reshape(n_rep, hot_rep, LANES)
    tally = dot(hot_table, jnp.ones((rows, n_hot), jnp.bfloat16))
    hnum[...] = diagonal(tally)
    rhpart[my] = hpart[my]
    rhnum[my] = hnum[...]
    pack(1)
    for step in range(1, n_rep):
        o = rep_at(step)
        to_rep(hpart.at[o], rhpart.at[my], 0, o)
        to_rep(hnum, rhnum.at[my], 1, o)
    for c in range(1, 4):
        each_owner(lambda o, c=c: to_owner(bucket.at[c, o], rbucket.at[c, me], 3 + c, o))

    arrived(rlabel, 2, n_own - 1)
    per = HALF // DEEP
    heaps = [jnp.sum(rlabel[j * per : (j + 1) * per], axis=0) for j in range(n_own // per)]
    if len(heaps) == 1:
        wide = [heaps[0][:, :HALF], heaps[0][:, HALF:]]
    else:
        wide = []
        for at_lane in (0, HALF):
            both = [h[:, at_lane : at_lane + HALF] for h in heaps]
            wide.append(jnp.concatenate(both, axis=1))

    @pl.loop(0, n_rep)
    def _(b):
        lines = iota((per_rep, slots), 0) + b * per_rep + 1
        for v in range(2):
            hit = ones_where(lines == wide[v]).astype(jnp.bfloat16)
            hits_of[b, v * per_rep : (v + 1) * per_rep] = hit
        tally = dot(hits_of[b], jnp.ones((slots, per_rep), jnp.bfloat16))
        count[b] = diagonal(tally[:per_rep] + tally[per_rep:])

    rcount[my] = count[my]
    for step in range(1, n_rep):
        o = rep_at(step)
        to_rep(count.at[o], rcount.at[my], 9, o)

    def add_up(c):
        arrived(rbucket.at[c], 3 + c, n_own - 1)
        high, lo = two_parts(rbucket[c].reshape(slots, LANES))
        rhs[:, :LANES] = high
        rhs[:, LANES:] = lo
        near = n_rep // 2

        def block(b):
            sums = folded(dot(hits_of[b], rhs[...]))
            a, z = sums[:per_rep], sums[per_rep:]
            if c % 2:
                a, z = z, a
            half = per_rep // 2
            straight = left_half(a[:half], z[half:])
            dense[c, b] = straight + turned(left_half(a[half:], z[:half]))

        def pair(j):
            return rep_at(j), lax.rem(my + n_rep - lax.rem(j, near), n_rep)

        def ship(j):
            a, b = pair(j)
            to_rep(dense.at[c, a], rdense.at[c, my], 10 + c, a)

            @pl.when(j < near)
            def _():
                to_rep(dense.at[c, b], rdense.at[c, my], 10 + c, b)

        @pl.loop(0, near)
        def _(i):
            a, b = pair(near - i)
            block(a)
            block(b)

            @pl.when(i > 0)
            def _():
                ship(near - i + 1)

        rdense[c, my] = dense[c, my]
        ship(1)

    add_up(0)

    arrived(rhpart, 0, n_rep - 1)
    arrived(rhnum, 1, n_rep - 1)
    hsum = jnp.sum(rhpart[...], axis=0)
    num = jnp.sum(rhnum[...], axis=0)
    mine = iota((hot_rep, n_hot), 1) == iota((hot_rep, n_hot), 0) + my * hot_rep
    num = jnp.sum(jnp.where(mine, num, 0.0), axis=1, keepdims=True)
    num = jnp.broadcast_to(num, (hot_rep, LANES)).reshape(hot_rep, 1, LANES)
    for h in range(2):
        block = hsum[:, h * LANES : (h + 1) * LANES].reshape(hot_rep, 1, LANES)
        piece[h * hot_rep : (h + 1) * hot_rep, :, :LANES] = block
        piece[h * hot_rep : (h + 1) * hot_rep, :, LANES:] = num
    rpiece[me] = piece[me]
    each_owner(lambda o: to_owner(piece.at[o], rpiece.at[me], 7, o))

    for c in range(1, 4):
        add_up(c)

    arrived(rpiece, 7, n_own - 1)
    total = jnp.sum(rpiece[...], axis=0)
    done[:, :LANES] = total[:, :LANES] / jnp.sqrt(1.0 + total[:, LANES:])
    done[:, LANES:] = total[:, LANES:]
    rdone[me] = done[...]
    each_owner(lambda o: to_owner(done, rdone.at[me], 8, o))

    arrived(rcount, 9, n_rep - 1)
    num = jnp.sum(rcount[...], axis=0)
    gcount[...] = num
    root = jnp.broadcast_to(jnp.sqrt(1.0 + column(num)), (per_rep, LANES))
    half = per_rep // 2
    root = left_half(root[:half], root[half:])

    def finish(t):
        whole = []
        for c in (2 * t, 2 * t + 1):
            arrived(rdense.at[c], 10 + c, n_rep - 1)
            whole.append(jnp.sum(rdense[c], axis=0) / root)
        a, b = whole
        gout[:half, t * LANES : (t + 1) * LANES] = left_half(a, turned(b))
        gout[half:, t * LANES : (t + 1) * LANES] = left_half(turned(a), b)

    finish(0)
    left(rhpart, 0, n_rep - 1)
    left(rhnum, 1, n_rep - 1)
    left(rlabel, 2, n_own - 1)
    for c in range(4):
        left(rbucket.at[c], 3 + c, n_own - 1)
    left(rpiece, 7, n_own - 1)

    arrived(rdone, 8, n_own - 1)
    for h in range(2):
        block = rdone[h * hot_rep : (h + 1) * hot_rep, :, :LANES]
        hout[:, h * LANES : (h + 1) * LANES] = block.reshape(hot_rep, LANES)
    tally = rdone[:hot_rep, :, LANES : LANES + hot_rep].reshape(hot_rep, hot_rep)
    hcount[...] = diagonal(tally)

    left(rdone, 8, n_own - 1)
    left(rcount, 9, n_rep - 1)
    finish(1)
    for c in range(4):
        left(rdense.at[c], 10 + c, n_rep - 1)


def write(*refs):
    sources, targets, sem = refs[:4], refs[4:8], refs[8]
    copies = [pltpu.make_async_copy(s, t, sem.at[i]) for i, (s, t) in enumerate(zip(sources, targets))]
    for copy in copies:
        copy.start()
    for copy in copies:
        copy.wait()


def local(n_own, n_rep, features, group_ids, survive, home_row, hot_ids):
    rows, width = features.shape
    groups, n_hot = home_row.shape[0], hot_ids.shape[0]
    own_groups = groups // n_own
    per_rep, hot_rep = own_groups // n_rep, n_hot // n_rep
    slots = n_own * DEEP
    f32, i32, bf16 = jnp.float32, jnp.int32, jnp.bfloat16
    vmem = pl.BlockSpec(memory_space=pltpu.VMEM)
    hbm = pl.BlockSpec(memory_space=pltpu.HBM)
    shapes = (
        jax.ShapeDtypeStruct((per_rep, width), f32),
        jax.ShapeDtypeStruct((1, per_rep), f32),
        jax.ShapeDtypeStruct((hot_rep, width), f32),
        jax.ShapeDtypeStruct((1, hot_rep), f32),
    )
    outs = pl.pallas_call(
        functools.partial(kernel, (n_own, n_rep, own_groups, n_hot)),
        out_shape=shapes,
        in_specs=[hbm] * 5,
        out_specs=(vmem,) * 4,
        scratch_shapes=[
            pltpu.VMEM((1, rows), i32),
            pltpu.VMEM((1, rows), i32),
            pltpu.VMEM((1, n_hot), i32),
            pltpu.VMEM((rows, width), f32),
            pltpu.VMEM((groups // LANES, LANES), i32),
            pltpu.VMEM((2, 2, rows, 2 * LANES), bf16),
            pltpu.VMEM((4, n_own, DEEP, LANES), f32),
            pltpu.VMEM((4, n_own, DEEP, LANES), f32),
            pltpu.VMEM((n_own, 1, LANES), i32),
            pltpu.VMEM((n_own, 1, LANES), i32),
            pltpu.VMEM((n_rep, 2 * per_rep, slots), bf16),
            pltpu.VMEM((slots, 2 * LANES), bf16),
            pltpu.VMEM((4, n_rep, per_rep // 2, LANES), f32),
            pltpu.VMEM((4, n_rep, per_rep // 2, LANES), f32),
            pltpu.VMEM((n_rep, 1, per_rep), f32),
            pltpu.VMEM((n_rep, 1, per_rep), f32),
            pltpu.VMEM((n_rep, hot_rep, width), f32),
            pltpu.VMEM((n_rep, hot_rep, width), f32),
            pltpu.VMEM((1, n_hot), f32),
            pltpu.VMEM((n_rep, 1, n_hot), f32),
            pltpu.VMEM((n_own, 1, 2 * LANES), f32),
            pltpu.VMEM((n_own, 1, 2 * LANES), f32),
            pltpu.VMEM((1, 2 * LANES), f32),
            pltpu.VMEM((n_own, 1, 2 * LANES), f32),
            pltpu.SemaphoreType.DMA((5,)),
            pltpu.SemaphoreType.DMA((14,)),
            pltpu.SemaphoreType.DMA((14,)),
        ],
        compiler_params=pltpu.CompilerParams(
            collective_id=0, has_side_effects=True, vmem_limit_bytes=67043328
        ),
    )(
        group_ids.reshape(1, rows),
        survive.reshape(1, rows),
        hot_ids.reshape(1, n_hot),
        features,
        home_row.reshape(groups // LANES, LANES),
    )
    gout, gcount, hout, hcount = pl.pallas_call(
        write,
        out_shape=shapes,
        in_specs=[vmem] * 4,
        out_specs=(hbm,) * 4,
        scratch_shapes=[pltpu.SemaphoreType.DMA((4,))],
    )(*outs)
    return gout, gcount.reshape(per_rep), hout, hcount.reshape(hot_rep)


def solution(mesh):
    return jax.shard_map(
        functools.partial(local, mesh.shape["owner"], mesh.shape["rep"]),
        mesh=mesh,
        in_specs=(P(OWNER_REP, None), P(OWNER_REP), P(OWNER_REP), P(), P()),
        out_specs=(P(OWNER_REP, None), P(OWNER_REP), P("rep", None), P("rep")),
        check_vma=False,
    )
```

time: 68.1 us -> 57.6 us (0.85); the launches traced: 66.8 us -> 57.5 us
  local copies, waits for them, and re-layouts: 4.97 us -> 0 us
  Pallas kernels: 61.2 us -> 56.8 us
    pallas_call x1, Pallas kernels: 61.2 us -> 55.2 us  [local(): pl.pallas_call(functools.partial(kernel, (n_own, n_rep, own_groups, n_hot...]
    unnamed x14 -> x0, local copies, waits for them, and re-layouts: 4.97 us -> none
    pallas_call x0 -> x1, Pallas kernels: none -> 1.61 us  [local(): pl.pallas_call(write, out_shape=shapes, in_specs=[vmem] * 4, out_specs=(h...]
where the time goes in v2:
time: 57.6 us; the launch traced here: 57.5 us
  Pallas kernels  56.8 us (99%)
  between operations  0.64 us (1%)
    pallas_call x1, Pallas kernels, local(): pl.pallas_call(functools.partial(kernel, (n_own, n_rep, own_groups, n_hot...  55.2 us
    pallas_call x1, Pallas kernels, local(): pl.pallas_call(write, out_shape=shapes, in_specs=[vmem] * 4, out_specs=(h...  1.61 us

profile of v2, /device:TPU:1, one launch (start us, length us, event | category | flops | bytes accessed | tf_op | source)
XLA Modules:
  0.0 57.5 jit_solution(7651927624190793325)
XLA Ops:
  0.6 55.2 %shard_map.84 = (f32[128,256]{1,0:T(8,128)}, f32[1,128]{1,0:T(1,128)}, f32[32,256]{1,0:T(8,128)}, f32[1,32]{1,0:T(1,128)}) custom-call(s32[1,512]{1,0:T(1,128)} %bitcast.7, s32[1,512]{1,0:T(1,128)} %bitcast.8, s32[1,256]{1,0:T(1,128)} %bitcast.9, f32[512,256]{1,0:T(8,128)} %feat_hbm.1, s32[512,128]{1,0:T(8,128)} %bitcast.6), custom_call_target="tpu_custom_call" | custom-call | tf_op jit(solution)/shard_map/pallas_call | solution.py:429
  55.9 1.6 %shard_map.85 = (f32[128,256]{1,0:T(8,128)}, f32[1,128]{1,0:T(1,128)}, f32[32,256]{1,0:T(8,128)}, f32[1,32]{1,0:T(1,128)}) custom-call(f32[128,256]{1,0:T(8,128)} %get-tuple-element.12.refs_0_, f32[1,128]{1,0:T(1,128)} %get-tuple-element.13.refs_1_, f32[32,256]{1,0:T(8,128)} %get-tuple-element.14.refs_2_, f32[1,32]{1,0:T(1,128)} %get-tuple-element.15.refs_3_), custom_call_target="tpu_custom_call" | custom-call | tf_op jit(solution)/shard_map/pallas_call | solution.py:473

commit v3 on v2

--- a/solution.py
+++ b/solution.py
@@ -10,10 +10,16 @@
 OWNER_REP = ("owner", "rep")
 MESH = pl.DeviceIdType.MESH
 LANES = 128
-HALF = 64
 CAP = 16
-DEEP = 8
+FOLD = 4
+DEEP = CAP // FOLD
+WIDE = LANES // FOLD
+CHUNKS = 2 * FOLD
 INNER = 8
+
+
+CH = 6
+RE = CH + CHUNKS
 
 
 def iota(shape, dim):
@@ -51,12 +57,17 @@
     )
 
 
-def left_half(a, b):
-    return jnp.where(iota(a.shape, 1) < HALF, a, b)
-
-
-def turned(x):
-    return pltpu.roll(x, HALF, 1)
+def woven(arrays):
+    lane = iota(arrays[0].shape, 1)
+    out = arrays[-1]
+    for i in range(FOLD - 2, -1, -1):
+        out = jnp.where(lane < (i + 1) * WIDE, arrays[i], out)
+    return out
+
+
+def turned(x, parts):
+    parts %= FOLD
+    return pltpu.roll(x, parts * WIDE, 1) if parts else x
 
 
 def kernel(
@@ -106,24 +117,24 @@
     slots = n_own * DEEP
     me = lax.axis_index("owner")
     my = lax.axis_index("rep")
-    zs = []
-    for k in range(n_z):
-        dz = ((k + 1) // 2) * (1 - 2 * (k % 2))
-        zs.append(lax.rem(lax.div(me, INNER) + (dz + n_z), n_z) * INNER)
-    x_me, c_me = lax.div(lax.rem(me, INNER), 2), lax.rem(me, 2)
+    z_me, x_me, c_me = lax.div(me, INNER), lax.div(lax.rem(me, INNER), 2), lax.rem(me, 2)
+    inner = []
+    for dx in (2, 1, 3, 0):
+        for dc in (1, 0):
+            inner.append(lax.rem(x_me + dx, INNER // 2) * 2 + lax.rem(c_me + dc, 2))
 
     def each_owner(act):
-        @pl.loop(0, INNER)
-        def _(m):
-            inner = lax.rem(x_me + lax.div(m, 2), INNER // 2) * 2 + lax.rem(c_me + m, 2)
-            for k in range(n_z):
-                if k == 0:
-
-                    @pl.when(m > 0)
-                    def _():
-                        act(zs[0] + inner)
-                else:
-                    act(zs[k] + inner)
+        @pl.loop(0, n_z)
+        def _(k):
+            far = n_z // 2 - lax.div(k + 1, 2)
+            dz = far * (2 * lax.rem(k, 2) - 1)
+            z = lax.rem(z_me + dz + n_z, n_z) * INNER
+            for o in inner[:-1]:
+                act(z + o)
+
+            @pl.when(k < n_z - 1)
+            def _():
+                act(z + inner[-1])
 
     def rep_at(step):
         return lax.rem(my + (step + n_rep), n_rep)
@@ -184,12 +195,12 @@
     before = ones_where(iota((rows, rows), 0) < iota((rows, rows), 1)).astype(jnp.bfloat16)
     earlier = dot(member.astype(jnp.bfloat16), before)
     pos = jnp.sum(member * earlier, axis=0, keepdims=True).astype(jnp.int32)
-    deep = pos >= DEEP
-    slot_a = jnp.where(jnp.logical_and(keep, jnp.logical_not(deep)), owner * DEEP + pos, -1)
-    slot_b = jnp.where(jnp.logical_and(keep, deep), owner * DEEP + pos - DEEP, -1)
-
-    shift = lax.rem(me, HALF // DEEP) * DEEP
-    place = jnp.where(deep, pos + (HALF - DEEP), pos) + shift
+    layer, depth = pos // DEEP, pos % DEEP
+    slot = [
+        jnp.where(jnp.logical_and(keep, layer == q), owner * DEEP + depth, -1) for q in range(FOLD)
+    ]
+
+    place = layer * WIDE + depth + lax.rem(me, WIDE // DEEP) * DEEP
     at = ones_where(iota((LANES, rows), 0) == place).astype(jnp.bfloat16)
     two = jnp.concatenate(
         [member * (local >> 5).astype(jnp.float32), member * (local & 31).astype(jnp.float32)],
@@ -201,27 +212,29 @@
     rlabel[me] = label[me]
 
     copies[4].wait()
-    for t in range(2):
+
+    def pack(t):
         block = feat[:, t * LANES : (t + 1) * LANES]
-        for v in range(2):
-            high, lo = two_parts(turned(block) if v else block)
-            parts[t, v, :, :LANES] = high
-            parts[t, v, :, LANES:] = lo
-
-    tall = min(256, slots)
-
-    def pack(t):
+        for q in range(FOLD):
+            high, lo = two_parts(turned(block, q))
+            parts[t, q, :, :LANES] = high
+            parts[t, q, :, LANES:] = lo
+        tall = min(128, slots)
+
         @pl.loop(0, slots // tall)
         def _(j):
             lines = iota((tall, rows), 0) + j * tall
-            a = folded(dot(ones_where(lines == slot_a).astype(jnp.bfloat16), parts[t, 0]))
-            b = folded(dot(ones_where(lines == slot_b).astype(jnp.bfloat16), parts[t, 1]))
+            packed = []
+            for q in range(FOLD):
+                chosen = ones_where(lines == slot[q]).astype(jnp.bfloat16)
+                packed.append(folded(dot(chosen, parts[t, q])))
             to = pl.ds(j * (tall // DEEP), tall // DEEP)
-            bucket[2 * t, to] = left_half(a, b).reshape(tall // DEEP, DEEP, LANES)
-            bucket[2 * t + 1, to] = left_half(b, a).reshape(tall // DEEP, DEEP, LANES)
-
-        for c in (2 * t, 2 * t + 1):
-            rbucket[c, me] = bucket[c, me]
+            for k in range(FOLD):
+                message = woven([packed[(i - k) % FOLD] for i in range(FOLD)])
+                bucket[t * FOLD + k, to] = message.reshape(tall // DEEP, DEEP, LANES)
+
+        for k in range(FOLD):
+            rbucket[t * FOLD + k, me] = bucket[t * FOLD + k, me]
 
     def to_owner(src, dst, which, o):
         pltpu.make_async_remote_copy(
@@ -252,12 +265,11 @@
     pack(0)
     pl.semaphore_wait(barrier, n_own - 1 + n_rep - 1)
 
-    def send_first(o):
-        to_owner(label.at[o], rlabel.at[me], 2, o)
-        to_owner(bucket.at[0, o], rbucket.at[0, me], 3, o)
-
-    each_owner(send_first)
-
+    each_owner(lambda o: to_owner(label.at[o], rlabel.at[me], 2, o))
+    for c in range(2):
+        each_owner(lambda o, c=c: to_owner(bucket.at[c, o], rbucket.at[c, me], CH + c, o))
+
+    pack(1)
     for t in range(2):
         part = folded(dot(hot_table, parts[t, 0]))
         hpart[:, :, t * LANES : (t + 1) * LANES] = part.reshape(n_rep, hot_rep, LANES)
@@ -265,41 +277,42 @@
     hnum[...] = diagonal(tally)
     rhpart[my] = hpart[my]
     rhnum[my] = hnum[...]
-    pack(1)
     for step in range(1, n_rep):
         o = rep_at(step)
         to_rep(hpart.at[o], rhpart.at[my], 0, o)
         to_rep(hnum, rhnum.at[my], 1, o)
-    for c in range(1, 4):
-        each_owner(lambda o, c=c: to_owner(bucket.at[c, o], rbucket.at[c, me], 3 + c, o))
+    for c in range(2, CHUNKS):
+        each_owner(lambda o, c=c: to_owner(bucket.at[c, o], rbucket.at[c, me], CH + c, o))
 
     arrived(rlabel, 2, n_own - 1)
-    per = HALF // DEEP
+    per = WIDE // DEEP
     heaps = [jnp.sum(rlabel[j * per : (j + 1) * per], axis=0) for j in range(n_own // per)]
-    if len(heaps) == 1:
-        wide = [heaps[0][:, :HALF], heaps[0][:, HALF:]]
-    else:
-        wide = []
-        for at_lane in (0, HALF):
-            both = [h[:, at_lane : at_lane + HALF] for h in heaps]
-            wide.append(jnp.concatenate(both, axis=1))
+    wide = []
+    for q in range(FOLD):
+        some = [h[:, q * WIDE : (q + 1) * WIDE] for h in heaps]
+        wide.append(some[0] if len(some) == 1 else jnp.concatenate(some, axis=1))
 
     @pl.loop(0, n_rep)
     def _(b):
         lines = iota((per_rep, slots), 0) + b * per_rep + 1
-        for v in range(2):
-            hit = ones_where(lines == wide[v]).astype(jnp.bfloat16)
-            hits_of[b, v * per_rep : (v + 1) * per_rep] = hit
-        tally = dot(hits_of[b], jnp.ones((slots, per_rep), jnp.bfloat16))
-        count[b] = diagonal(tally[:per_rep] + tally[per_rep:])
-
-    rcount[my] = count[my]
-    for step in range(1, n_rep):
-        o = rep_at(step)
-        to_rep(count.at[o], rcount.at[my], 9, o)
+        for q in range(FOLD):
+            hit = ones_where(lines == wide[q]).astype(jnp.bfloat16)
+            hits_of[b, q * per_rep : (q + 1) * per_rep] = hit
+
+    def count_up():
+        @pl.loop(0, n_rep)
+        def _(b):
+            tally = dot(hits_of[b], jnp.ones((slots, per_rep), jnp.bfloat16))
+            tally = sum(tally[q * per_rep : (q + 1) * per_rep] for q in range(FOLD))
+            count[b] = diagonal(tally)
+
+        rcount[my] = count[my]
+        for step in range(1, n_rep):
+            o = rep_at(step)
+            to_rep(count.at[o], rcount.at[my], 5, o)
 
     def add_up(c):
-        arrived(rbucket.at[c], 3 + c, n_own - 1)
+        arrived(rbucket.at[c], CH + c, n_own - 1)
         high, lo = two_parts(rbucket[c].reshape(slots, LANES))
         rhs[:, :LANES] = high
         rhs[:, LANES:] = lo
@@ -307,38 +320,35 @@
 
         def block(b):
             sums = folded(dot(hits_of[b], rhs[...]))
-            a, z = sums[:per_rep], sums[per_rep:]
-            if c % 2:
-                a, z = z, a
-            half = per_rep // 2
-            straight = left_half(a[:half], z[half:])
-            dense[c, b] = straight + turned(left_half(a[half:], z[:half]))
-
-        def pair(j):
-            return rep_at(j), lax.rem(my + n_rep - lax.rem(j, near), n_rep)
-
-        def ship(j):
-            a, b = pair(j)
-            to_rep(dense.at[c, a], rdense.at[c, my], 10 + c, a)
-
-            @pl.when(j < near)
-            def _():
-                to_rep(dense.at[c, b], rdense.at[c, my], 10 + c, b)
-
-        @pl.loop(0, near)
-        def _(i):
-            a, b = pair(near - i)
-            block(a)
-            block(b)
-
-            @pl.when(i > 0)
-            def _():
-                ship(near - i + 1)
-
+            low = per_rep // FOLD
+            total = None
+            for shift in range(FOLD):
+                terms = []
+                for i in range(FOLD):
+                    start = ((i - c) % FOLD) * per_rep + ((i + shift) % FOLD) * low
+                    terms.append(sums[start : start + low])
+                term = turned(woven(terms), shift)
+                total = term if total is None else total + term
+            dense[c, b] = total
+
+        def target(i):
+            far = near - lax.div(i, 2)
+            return lax.rem(my + n_rep + far * (1 - 2 * lax.rem(i, 2)), n_rep)
+
+        def ship(i):
+            o = target(i)
+            to_rep(dense.at[c, o], rdense.at[c, my], RE + c, o)
+
+        for i in range(1, n_rep):
+            block(target(i))
+        block(my)
+        for i in range(1, n_rep):
+            ship(i)
         rdense[c, my] = dense[c, my]
-        ship(1)
 
     add_up(0)
+    count_up()
+    add_up(1)
 
     arrived(rhpart, 0, n_rep - 1)
     arrived(rhnum, 1, n_rep - 1)
@@ -346,60 +356,63 @@
     num = jnp.sum(rhnum[...], axis=0)
     mine = iota((hot_rep, n_hot), 1) == iota((hot_rep, n_hot), 0) + my * hot_rep
     num = jnp.sum(jnp.where(mine, num, 0.0), axis=1, keepdims=True)
-    num = jnp.broadcast_to(num, (hot_rep, LANES)).reshape(hot_rep, 1, LANES)
+    across = iota((hot_rep, LANES), 0) == iota((hot_rep, LANES), 1)
+    num = jnp.sum(jnp.where(across, num, 0.0), axis=0, keepdims=True)
+    piece[:, :, LANES:] = jnp.broadcast_to(num.reshape(1, 1, LANES), (n_own, 1, LANES))
     for h in range(2):
         block = hsum[:, h * LANES : (h + 1) * LANES].reshape(hot_rep, 1, LANES)
         piece[h * hot_rep : (h + 1) * hot_rep, :, :LANES] = block
-        piece[h * hot_rep : (h + 1) * hot_rep, :, LANES:] = num
     rpiece[me] = piece[me]
-    each_owner(lambda o: to_owner(piece.at[o], rpiece.at[me], 7, o))
-
-    for c in range(1, 4):
+    each_owner(lambda o: to_owner(piece.at[o], rpiece.at[me], 3, o))
+
+    for c in range(2, CHUNKS):
         add_up(c)
 
-    arrived(rpiece, 7, n_own - 1)
+    arrived(rpiece, 3, n_own - 1)
     total = jnp.sum(rpiece[...], axis=0)
-    done[:, :LANES] = total[:, :LANES] / jnp.sqrt(1.0 + total[:, LANES:])
-    done[:, LANES:] = total[:, LANES:]
+    done[...] = total[:, :LANES]
+    hot_num = total[:, LANES:]
     rdone[me] = done[...]
-    each_owner(lambda o: to_owner(done, rdone.at[me], 8, o))
-
-    arrived(rcount, 9, n_rep - 1)
+    each_owner(lambda o: to_owner(done, rdone.at[me], 4, o))
+
+    arrived(rcount, 5, n_rep - 1)
     num = jnp.sum(rcount[...], axis=0)
     gcount[...] = num
     root = jnp.broadcast_to(jnp.sqrt(1.0 + column(num)), (per_rep, LANES))
-    half = per_rep // 2
-    root = left_half(root[:half], root[half:])
+    low = per_rep // FOLD
+    root = woven([root[g * low : (g + 1) * low] for g in range(FOLD)])
 
     def finish(t):
         whole = []
-        for c in (2 * t, 2 * t + 1):
-            arrived(rdense.at[c], 10 + c, n_rep - 1)
+        for k in range(FOLD):
+            c = t * FOLD + k
+            arrived(rdense.at[c], RE + c, n_rep - 1)
             whole.append(jnp.sum(rdense[c], axis=0) / root)
-        a, b = whole
-        gout[:half, t * LANES : (t + 1) * LANES] = left_half(a, turned(b))
-        gout[half:, t * LANES : (t + 1) * LANES] = left_half(turned(a), b)
+        for g in range(FOLD):
+            block = woven([turned(whole[k], k - g) for k in range(FOLD)])
+            gout[g * low : (g + 1) * low, t * LANES : (t + 1) * LANES] = block
 
     finish(0)
     left(rhpart, 0, n_rep - 1)
     left(rhnum, 1, n_rep - 1)
     left(rlabel, 2, n_own - 1)
-    for c in range(4):
-        left(rbucket.at[c], 3 + c, n_own - 1)
-    left(rpiece, 7, n_own - 1)
-
-    arrived(rdone, 8, n_own - 1)
+    for c in range(CHUNKS):
+        left(rbucket.at[c], CH + c, n_own - 1)
+    left(rpiece, 3, n_own - 1)
+
+    arrived(rdone, 4, n_own - 1)
+    hot_root = jnp.sum(jnp.where(across, hot_num, 0.0), axis=1, keepdims=True)
+    hot_root = jnp.sqrt(1.0 + hot_root)
     for h in range(2):
-        block = rdone[h * hot_rep : (h + 1) * hot_rep, :, :LANES]
-        hout[:, h * LANES : (h + 1) * LANES] = block.reshape(hot_rep, LANES)
-    tally = rdone[:hot_rep, :, LANES : LANES + hot_rep].reshape(hot_rep, hot_rep)
-    hcount[...] = diagonal(tally)
-
-    left(rdone, 8, n_own - 1)
-    left(rcount, 9, n_rep - 1)
+        block = rdone[h * hot_rep : (h + 1) * hot_rep].reshape(hot_rep, LANES)
+        hout[:, h * LANES : (h + 1) * LANES] = block / hot_root
+    hcount[...] = hot_num[:, :hot_rep]
+
+    left(rdone, 4, n_own - 1)
+    left(rcount, 5, n_rep - 1)
     finish(1)
-    for c in range(4):
-        left(rdense.at[c], 10 + c, n_rep - 1)
+    for c in range(CHUNKS):
+        left(rdense.at[c], RE + c, n_rep - 1)
 
 
 def write(*refs):
@@ -437,15 +450,15 @@
             pltpu.VMEM((1, n_hot), i32),
             pltpu.VMEM((rows, width), f32),
             pltpu.VMEM((groups // LANES, LANES), i32),
-            pltpu.VMEM((2, 2, rows, 2 * LANES), bf16),
-            pltpu.VMEM((4, n_own, DEEP, LANES), f32),
-            pltpu.VMEM((4, n_own, DEEP, LANES), f32),
+            pltpu.VMEM((2, FOLD, rows, 2 * LANES), bf16),
+            pltpu.VMEM((CHUNKS, n_own, DEEP, LANES), f32),
+            pltpu.VMEM((CHUNKS, n_own, DEEP, LANES), f32),
             pltpu.VMEM((n_own, 1, LANES), i32),
             pltpu.VMEM((n_own, 1, LANES), i32),
-            pltpu.VMEM((n_rep, 2 * per_rep, slots), bf16),
+            pltpu.VMEM((n_rep, FOLD * per_rep, slots), bf16),
             pltpu.VMEM((slots, 2 * LANES), bf16),
-            pltpu.VMEM((4, n_rep, per_rep // 2, LANES), f32),
-            pltpu.VMEM((4, n_rep, per_rep // 2, LANES), f32),
+            pltpu.VMEM((CHUNKS, n_rep, per_rep // FOLD, LANES), f32),
+            pltpu.VMEM((CHUNKS, n_rep, per_rep // FOLD, LANES), f32),
             pltpu.VMEM((n_rep, 1, per_rep), f32),
             pltpu.VMEM((n_rep, 1, per_rep), f32),
             pltpu.VMEM((n_rep, hot_rep, width), f32),
@@ -454,11 +467,11 @@
             pltpu.VMEM((n_rep, 1, n_hot), f32),
             pltpu.VMEM((n_own, 1, 2 * LANES), f32),
             pltpu.VMEM((n_own, 1, 2 * LANES), f32),
-            pltpu.VMEM((1, 2 * LANES), f32),
-            pltpu.VMEM((n_own, 1, 2 * LANES), f32),
+            pltpu.VMEM((1, LANES), f32),
+            pltpu.VMEM((n_own, 1, LANES), f32),
             pltpu.SemaphoreType.DMA((5,)),
-            pltpu.SemaphoreType.DMA((14,)),
-            pltpu.SemaphoreType.DMA((14,)),
+            pltpu.SemaphoreType.DMA((RE + CHUNKS,)),
+            pltpu.SemaphoreType.DMA((RE + CHUNKS,)),
         ],
         compiler_params=pltpu.CompilerParams(
             collective_id=0, has_side_effects=True, vmem_limit_bytes=67043328

time: 57.6 us -> 53 us (0.920)
  Pallas kernels: 56.8 us -> 52.2 us
    pallas_call x1, Pallas kernels: 55.2 us -> 50.6 us  [local(): pl.pallas_call(functools.partial(kernel, (n_own, n_rep, own_groups, n_hot...]
where the time goes in v3:
time: 53 us; the launch traced here: 52.9 us
  Pallas kernels  52.2 us (98%)
  between operations  0.64 us (1%)
    pallas_call x1, Pallas kernels, local(): pl.pallas_call(functools.partial(kernel, (n_own, n_rep, own_groups, n_hot...  50.6 us
    pallas_call x1, Pallas kernels, local(): pl.pallas_call(write, out_shape=shapes, in_specs=[vmem] * 4, out_specs=(h...  1.61 us

profile of v3, /device:TPU:1, one launch (start us, length us, event | category | flops | bytes accessed | tf_op | source)
XLA Modules:
  0.0 52.9 jit_solution(9469593872299108146)
XLA Ops:
  0.6 50.6 %shard_map.84 = (f32[128,256]{1,0:T(8,128)}, f32[1,128]{1,0:T(1,128)}, f32[32,256]{1,0:T(8,128)}, f32[1,32]{1,0:T(1,128)}) custom-call(s32[1,512]{1,0:T(1,128)} %bitcast.7, s32[1,512]{1,0:T(1,128)} %bitcast.8, s32[1,256]{1,0:T(1,128)} %bitcast.9, f32[512,256]{1,0:T(8,128)} %feat_hbm.1, s32[512,128]{1,0:T(8,128)} %bitcast.6), custom_call_target="tpu_custom_call" | custom-call | tf_op jit(solution)/shard_map/pallas_call | solution.py:442
  51.3 1.6 %shard_map.85 = (f32[128,256]{1,0:T(8,128)}, f32[1,128]{1,0:T(1,128)}, f32[32,256]{1,0:T(8,128)}, f32[1,32]{1,0:T(1,128)}) custom-call(f32[128,256]{1,0:T(8,128)} %get-tuple-element.12.refs_0_, f32[1,128]{1,0:T(1,128)} %get-tuple-element.13.refs_1_, f32[32,256]{1,0:T(8,128)} %get-tuple-element.14.refs_2_, f32[1,32]{1,0:T(1,128)} %get-tuple-element.15.refs_3_), custom_call_target="tpu_custom_call" | custom-call | tf_op jit(solution)/shard_map/pallas_call | solution.py:486

commit v4 on v3

--- a/solution.py
+++ b/solution.py
@@ -439,9 +439,16 @@
         jax.ShapeDtypeStruct((hot_rep, width), f32),
         jax.ShapeDtypeStruct((1, hot_rep), f32),
     )
+    given = (
+        group_ids.reshape(1, rows),
+        survive.reshape(1, rows),
+        hot_ids.reshape(1, n_hot),
+        features,
+        home_row.reshape(groups // LANES, LANES),
+    )
     outs = pl.pallas_call(
         functools.partial(kernel, (n_own, n_rep, own_groups, n_hot)),
-        out_shape=shapes,
+        out_shape=tuple(pltpu.VMEM(s.shape, s.dtype) for s in shapes),
         in_specs=[hbm] * 5,
         out_specs=(vmem,) * 4,
         scratch_shapes=[
@@ -474,14 +481,10 @@
             pltpu.SemaphoreType.DMA((RE + CHUNKS,)),
         ],
         compiler_params=pltpu.CompilerParams(
-            collective_id=0, has_side_effects=True, vmem_limit_bytes=67043328
+            collective_id=0, has_side_effects=True, vmem_limit_bytes=32 * 1024 * 1024
         ),
     )(
-        group_ids.reshape(1, rows),
-        survive.reshape(1, rows),
-        hot_ids.reshape(1, n_hot),
-        features,
-        home_row.reshape(groups // LANES, LANES),
+        *(pltpu.with_memory_space_constraint(a, pltpu.HBM) for a in given)
     )
     gout, gcount, hout, hcount = pl.pallas_call(
         write,
@@ -489,6 +492,7 @@
         in_specs=[vmem] * 4,
         out_specs=(hbm,) * 4,
         scratch_shapes=[pltpu.SemaphoreType.DMA((4,))],
+        compiler_params=pltpu.CompilerParams(vmem_limit_bytes=1024 * 1024),
     )(*outs)
     return gout, gcount.reshape(per_rep), hout, hcount.reshape(hot_rep)
 

time: 53 us -> 51.5 us (0.972)
  Pallas kernels: 52.2 us -> 50.7 us
    pallas_call x1, Pallas kernels: 1.61 us -> 0.7 us  [local(): pl.pallas_call(write, out_shape=shapes, in_specs=[vmem] * 4, out_specs=(h...]
    pallas_call x1, Pallas kernels: 50.6 us -> 50 us  [local(): pl.pallas_call(functools.partial(kernel, (n_own, n_rep, own_groups, n_hot...]
where the time goes in v4:
time: 51.5 us; the launch traced here: 51.3 us
  Pallas kernels  50.7 us (98%)
  between operations  0.64 us (1%)
    pallas_call x1, Pallas kernels, local(): pl.pallas_call(functools.partial(kernel, (n_own, n_rep, own_groups, n_hot...  50 us

profile of v4, /device:TPU:1, one launch (start us, length us, event | category | flops | bytes accessed | tf_op | source)
XLA Modules:
  0.0 51.3 jit_solution(10772095616763253994)
XLA Ops:
  0.6 50.0 %shard_map.84 = (f32[128,256]{1,0:T(8,128)S(1)}, f32[1,128]{1,0:T(1,128)S(1)}, f32[32,256]{1,0:T(8,128)S(1)}, f32[1,32]{1,0:T(1,128)S(1)}) custom-call(s32[1,512]{1,0:T(1,128)} %bitcast.7, s32[1,512]{1,0:T(1,128)} %bitcast.8, s32[1,256]{1,0:T(1,128)} %bitcast.9, f32[512,256]{1,0:T(8,128)} %feat_hbm.1, s32[512,128]{1,0:T(8,128)} %bitcast.6), custom_call_target="tpu_custom_call" | custom-call | tf_op jit(solution)/shard_map/pallas_call | solution.py:449
  50.6 0.7 %shard_map.85 = (f32[128,256]{1,0:T(8,128)}, f32[1,128]{1,0:T(1,128)}, f32[32,256]{1,0:T(8,128)}, f32[1,32]{1,0:T(1,128)}) custom-call(f32[128,256]{1,0:T(8,128)S(1)} %get-tuple-element.12.refs_0_, f32[1,128]{1,0:T(1,128)S(1)} %get-tuple-element.13.refs_1_, f32[32,256]{1,0:T(8,128)S(1)} %get-tuple-element.14.refs_2_, f32[1,32]{1,0:T(1,128)S(1)} %get-tuple-element.15.refs_3_), custom_call_target="tpu_custom_call" | custom-call | tf_op jit(solution)/shard_map/pallas_call | solution.py:489

commit v5 on v4

--- a/solution.py
+++ b/solution.py
@@ -18,7 +18,8 @@
 INNER = 8
 
 
-CH = 6
+FIRST = 3
+CH = 9
 RE = CH + CHUNKS
 
 
@@ -103,6 +104,12 @@
     rhnum,
     piece,
     rpiece,
+    rsome,
+    level,
+    rlevel,
+    some_num,
+    level_num,
+    rlevel_num,
     done,
     rdone,
     in_sem,
@@ -219,7 +226,7 @@
             high, lo = two_parts(turned(block, q))
             parts[t, q, :, :LANES] = high
             parts[t, q, :, LANES:] = lo
-        tall = min(128, slots)
+        tall = min(256, slots)
 
         @pl.loop(0, slots // tall)
         def _(j):
@@ -341,8 +348,11 @@
 
         for i in range(1, n_rep):
             block(target(i))
+            if c == CHUNKS - 1 and i == FIRST:
+                for k in range(1, FIRST + 1):
+                    ship(k)
         block(my)
-        for i in range(1, n_rep):
+        for i in range(FIRST + 1 if c == CHUNKS - 1 and FIRST < n_rep else 1, n_rep):
             ship(i)
         rdense[c, my] = dense[c, my]
 
@@ -357,23 +367,40 @@
     mine = iota((hot_rep, n_hot), 1) == iota((hot_rep, n_hot), 0) + my * hot_rep
     num = jnp.sum(jnp.where(mine, num, 0.0), axis=1, keepdims=True)
     across = iota((hot_rep, LANES), 0) == iota((hot_rep, LANES), 1)
-    num = jnp.sum(jnp.where(across, num, 0.0), axis=0, keepdims=True)
-    piece[:, :, LANES:] = jnp.broadcast_to(num.reshape(1, 1, LANES), (n_own, 1, LANES))
-    for h in range(2):
-        block = hsum[:, h * LANES : (h + 1) * LANES].reshape(hot_rep, 1, LANES)
-        piece[h * hot_rep : (h + 1) * hot_rep, :, :LANES] = block
-    rpiece[me] = piece[me]
-    each_owner(lambda o: to_owner(piece.at[o], rpiece.at[me], 3, o))
-
-    for c in range(2, CHUNKS):
+    some_num[...] = jnp.sum(jnp.where(across, num, 0.0), axis=0, keepdims=True)
+    piece[...] = hsum.reshape(piece.shape)
+    place = lax.rem(me, INNER)
+    rpiece[place] = piece[place]
+    rsome[place] = some_num[...]
+    for o in inner[:-1]:
+        to_owner(piece.at[o], rpiece.at[place], 3, z_me * INNER + o)
+        to_owner(some_num, rsome.at[place], 4, z_me * INNER + o)
+
+    add_up(2)
+    add_up(3)
+
+    arrived(rpiece, 3, INNER - 1)
+    arrived(rsome, 4, INNER - 1)
+    level[...] = jnp.sum(rpiece[...], axis=0)
+    level_num[...] = jnp.sum(rsome[...], axis=0)
+    rlevel[z_me] = level[...]
+    rlevel_num[z_me] = level_num[...]
+    for k in range(n_z - 1):
+        far = n_z // 2 - (k + 1) // 2
+        z = lax.rem(z_me + n_z + far * (2 * (k % 2) - 1), n_z)
+        to_owner(level, rlevel.at[z_me], 6, z * INNER + place)
+        to_owner(level_num, rlevel_num.at[z_me], 7, z * INNER + place)
+
+    for c in range(4, CHUNKS):
         add_up(c)
 
-    arrived(rpiece, 3, n_own - 1)
-    total = jnp.sum(rpiece[...], axis=0)
-    done[...] = total[:, :LANES]
-    hot_num = total[:, LANES:]
-    rdone[me] = done[...]
-    each_owner(lambda o: to_owner(done, rdone.at[me], 4, o))
+    arrived(rlevel, 6, n_z - 1)
+    arrived(rlevel_num, 7, n_z - 1)
+    hot_num = jnp.sum(rlevel_num[...], axis=0)
+    done[...] = jnp.sum(rlevel[...], axis=0)
+    rdone[place] = done[...]
+    for o in inner[:-1]:
+        to_owner(done, rdone.at[place], 8, z_me * INNER + o)
 
     arrived(rcount, 5, n_rep - 1)
     num = jnp.sum(rcount[...], axis=0)
@@ -398,17 +425,17 @@
     left(rlabel, 2, n_own - 1)
     for c in range(CHUNKS):
         left(rbucket.at[c], CH + c, n_own - 1)
-    left(rpiece, 3, n_own - 1)
-
-    arrived(rdone, 4, n_own - 1)
+    left(rpiece, 3, INNER - 1)
+    left(rsome, 4, INNER - 1)
+    left(rlevel, 6, n_z - 1)
+    left(rlevel_num, 7, n_z - 1)
+
+    arrived(rdone, 8, INNER - 1)
     hot_root = jnp.sum(jnp.where(across, hot_num, 0.0), axis=1, keepdims=True)
-    hot_root = jnp.sqrt(1.0 + hot_root)
-    for h in range(2):
-        block = rdone[h * hot_rep : (h + 1) * hot_rep].reshape(hot_rep, LANES)
-        hout[:, h * LANES : (h + 1) * LANES] = block / hot_root
+    hout[...] = rdone[...].reshape(hout.shape) / jnp.sqrt(1.0 + hot_root)
     hcount[...] = hot_num[:, :hot_rep]
 
-    left(rdone, 4, n_own - 1)
+    left(rdone, 8, INNER - 1)
     left(rcount, 5, n_rep - 1)
     finish(1)
     for c in range(CHUNKS):
@@ -429,7 +456,7 @@
     groups, n_hot = home_row.shape[0], hot_ids.shape[0]
     own_groups = groups // n_own
     per_rep, hot_rep = own_groups // n_rep, n_hot // n_rep
-    slots = n_own * DEEP
+    slots, share = n_own * DEEP, hot_rep // INNER
     f32, i32, bf16 = jnp.float32, jnp.int32, jnp.bfloat16
     vmem = pl.BlockSpec(memory_space=pltpu.VMEM)
     hbm = pl.BlockSpec(memory_space=pltpu.HBM)
@@ -472,10 +499,16 @@
             pltpu.VMEM((n_rep, hot_rep, width), f32),
             pltpu.VMEM((1, n_hot), f32),
             pltpu.VMEM((n_rep, 1, n_hot), f32),
-            pltpu.VMEM((n_own, 1, 2 * LANES), f32),
-            pltpu.VMEM((n_own, 1, 2 * LANES), f32),
+            pltpu.VMEM((INNER, share, width), f32),
+            pltpu.VMEM((INNER, share, width), f32),
+            pltpu.VMEM((INNER, 1, LANES), f32),
+            pltpu.VMEM((share, width), f32),
+            pltpu.VMEM((n_own // INNER, share, width), f32),
             pltpu.VMEM((1, LANES), f32),
-            pltpu.VMEM((n_own, 1, LANES), f32),
+            pltpu.VMEM((1, LANES), f32),
+            pltpu.VMEM((n_own // INNER, 1, LANES), f32),
+            pltpu.VMEM((share, width), f32),
+            pltpu.VMEM((INNER, share, width), f32),
             pltpu.SemaphoreType.DMA((5,)),
             pltpu.SemaphoreType.DMA((RE + CHUNKS,)),
             pltpu.SemaphoreType.DMA((RE + CHUNKS,)),

time: 51.5 us -> 51.4 us (level)
  no operation moved by 1% of the time
where the time goes in v5:
time: 51.4 us; the launch traced here: 51.3 us
  Pallas kernels  50.6 us (98%)
  between operations  0.64 us (1%)
    pallas_call x1, Pallas kernels, local(): pl.pallas_call(functools.partial(kernel, (n_own, n_rep, own_groups, n_hot...  49.9 us

profile of v5, /device:TPU:1, one launch (start us, length us, event | category | flops | bytes accessed | tf_op | source)
XLA Modules:
  0.0 51.3 jit_solution(9298498892311058073)
XLA Ops:
  0.6 49.9 %shard_map.84 = (f32[128,256]{1,0:T(8,128)S(1)}, f32[1,128]{1,0:T(1,128)S(1)}, f32[32,256]{1,0:T(8,128)S(1)}, f32[1,32]{1,0:T(1,128)S(1)}) custom-call(s32[1,512]{1,0:T(1,128)} %bitcast.7, s32[1,512]{1,0:T(1,128)} %bitcast.8, s32[1,256]{1,0:T(1,128)} %bitcast.9, f32[512,256]{1,0:T(8,128)} %feat_hbm.1, s32[512,128]{1,0:T(8,128)} %bitcast.6), custom_call_target="tpu_custom_call" | custom-call | tf_op jit(solution)/shard_map/pallas_call | solution.py:476
  50.6 0.7 %shard_map.85 = (f32[128,256]{1,0:T(8,128)}, f32[1,128]{1,0:T(1,128)}, f32[32,256]{1,0:T(8,128)}, f32[1,32]{1,0:T(1,128)}) custom-call(f32[128,256]{1,0:T(8,128)S(1)} %get-tuple-element.12.refs_0_, f32[1,128]{1,0:T(1,128)S(1)} %get-tuple-element.13.refs_1_, f32[32,256]{1,0:T(8,128)S(1)} %get-tuple-element.14.refs_2_, f32[1,32]{1,0:T(1,128)S(1)} %get-tuple-element.15.refs_3_), custom_call_target="tpu_custom_call" | custom-call | tf_op jit(solution)/shard_map/pallas_call | solution.py:522

commit v6 on v5

--- a/solution.py
+++ b/solution.py
@@ -18,7 +18,7 @@
 INNER = 8
 
 
-FIRST = 3
+FIRST = 1
 CH = 9
 RE = CH + CHUNKS
 
@@ -164,7 +164,11 @@
     def greet(o):
         pl.semaphore_signal(barrier, inc=1, device_id=(o, my), device_id_type=MESH)
 
-    each_owner(greet)
+    for k in range(n_z):
+        far = n_z // 2 - (k + 1) // 2
+        z = lax.rem(z_me + n_z + far * (2 * (k % 2) - 1), n_z) * INNER
+        for o in inner if k < n_z - 1 else inner[:-1]:
+            greet(z + o)
     for step in range(1, n_rep):
         pl.semaphore_signal(barrier, inc=1, device_id=(me, rep_at(step)), device_id_type=MESH)
 

time: 51.4 us -> 51.3 us (level)
  no operation moved by 1% of the time
where the time goes in v6:
time: 51.3 us; the launch traced here: 51.1 us
  Pallas kernels  50.5 us (98%)
  between operations  0.64 us (1%)
    pallas_call x1, Pallas kernels, local(): pl.pallas_call(functools.partial(kernel, (n_own, n_rep, own_groups, n_hot...  49.8 us

profile of v6, /device:TPU:1, one launch (start us, length us, event | category | flops | bytes accessed | tf_op | source)
XLA Modules:
  0.0 51.1 jit_solution(11493833947209066987)
XLA Ops:
  0.6 49.8 %shard_map.84 = (f32[128,256]{1,0:T(8,128)S(1)}, f32[1,128]{1,0:T(1,128)S(1)}, f32[32,256]{1,0:T(8,128)S(1)}, f32[1,32]{1,0:T(1,128)S(1)}) custom-call(s32[1,512]{1,0:T(1,128)} %bitcast.7, s32[1,512]{1,0:T(1,128)} %bitcast.8, s32[1,256]{1,0:T(1,128)} %bitcast.9, f32[512,256]{1,0:T(8,128)} %feat_hbm.1, s32[512,128]{1,0:T(8,128)} %bitcast.6), custom_call_target="tpu_custom_call" | custom-call | tf_op jit(solution)/shard_map/pallas_call | solution.py:480
  50.4 0.7 %shard_map.85 = (f32[128,256]{1,0:T(8,128)}, f32[1,128]{1,0:T(1,128)}, f32[32,256]{1,0:T(8,128)}, f32[1,32]{1,0:T(1,128)}) custom-call(f32[128,256]{1,0:T(8,128)S(1)} %get-tuple-element.12.refs_0_, f32[1,128]{1,0:T(1,128)S(1)} %get-tuple-element.13.refs_1_, f32[32,256]{1,0:T(8,128)S(1)} %get-tuple-element.14.refs_2_, f32[1,32]{1,0:T(1,128)S(1)} %get-tuple-element.15.refs_3_), custom_call_target="tpu_custom_call" | custom-call | tf_op jit(solution)/shard_map/pallas_call | solution.py:526
